TPU v7x, 512 devices: a whole 4x8x8 slice. The times are simulated.
512 devices in a mesh: lat: 16 (over y_lo, z), lon: 32 (over y_hi, x, core).
Axes of the slice: x: 4, y: 8 (y_hi: 4, y_lo: 2; y = y_hi * 2 + y_lo), z: 8, core: 2. Of those that a mesh axis runs over, the one named last changes fastest.
Arguments:
- state_grid: bfloat16 [96, 2688, 192], P('lat', 'lon'), may hold values from -6 to 6
- norm_gain: float32 [192], replicated, may hold values from 0.1 to 1.9
- w_qkv: bfloat16 [192, 576], replicated, may hold values from -0.4375 to 0.4375
- w_proj: bfloat16 [192, 192], replicated, may hold values from -1.25 to 1.25
- bias_table: float32 [8, 6, 253], replicated, may hold values from -6 to 300
- window_kind: int32 [16, 224], replicated, may hold values from 0 to 7
- cotangent: bfloat16 [96, 2688, 192], P('lat', 'lon'), may hold values from -6 to 6
Outputs:
- out_field: bfloat16 [96, 2688, 192], P('lat', 'lon')
- d_field: bfloat16 [96, 2688, 192], P('lat', 'lon')
- qkv_grad: float32 [192, 576], replicated
- proj_grad: float32 [192, 192], replicated
- table_grad: float32 [8, 6, 253], replicated
- gain_grad: float32 [192], replicated
All inputs are finite; a program needn't handle non-finite values.
Results may differ from a plain program's by a relative error of at most 0.009.
Values may be sent and summed in bfloat16 or wider, within the bound.
No kernel may reach another device: no remote copies, remote signals or barrier semaphores. Data moves between devices by JAX's collectives and lax.ppermute only.
A program may use at most 64 MiB of HBM per device.

v0:
```python
import jax
import jax.numpy as jnp
from jax import lax
from jax.sharding import PartitionSpec as P

HEADS = 6
WIN_LAT = 6
WIN_LON = 12


norm_eps = 1e-05
clip_eps = 1e-06
clip_level = 1.0
masked_score = -1e30
highest = lax.Precision.HIGHEST


def shifted(value, axis, steps):
    count = lax.axis_size(axis)
    pairs = [(source, (source + steps) % count) for source in range(count)]
    return lax.ppermute(value, axis, pairs)


def packed_total(arrays, axis):
    ends = [0]
    for a in arrays:
        ends.append(ends[-1] + a.size)
    so_far = lax.psum(jnp.concatenate([a.ravel() for a in arrays]), axis)
    return tuple((so_far[b:e].reshape(a.shape) for a, b, e in zip(arrays, ends, ends[1:])))


def relation_onehot(win_lat, win_lon):
    position = jnp.arange(win_lat * win_lon, dtype=jnp.int32)
    row_of = position // win_lon
    column = position % win_lon
    offset = (row_of[:, None] - row_of[None, :] + win_lat - 1) * (2 * win_lon - 1) + (
        column[:, None] - column[None, :] + win_lon - 1
    )
    extent = (2 * win_lat - 1) * (2 * win_lon - 1)
    return (offset.reshape(-1)[:, None] == jnp.arange(extent, dtype=jnp.int32)[None, :]).astype(
        jnp.float32
    )


def to_windows(source, win_lat, win_lon):
    rows_all, cols_all, channels = source.shape
    source = source.reshape(rows_all // win_lat, win_lat, cols_all // win_lon, win_lon, channels)
    return source.transpose(0, 2, 1, 3, 4).reshape(-1, win_lat * win_lon, channels)


def from_windows(windows, rows_all, cols_all, win_lat, win_lon):
    channels = windows.shape[-1]
    source = windows.reshape(rows_all // win_lat, cols_all // win_lon, win_lat, win_lon, channels)
    return source.transpose(0, 2, 1, 3, 4).reshape(rows_all, cols_all, channels)


def window_bias(bias_table, kinds_flat, onehot_rel, positions):
    kind_count, heads_n, extent = bias_table.shape
    spread = jnp.einsum(
        "ke,pe->kp",
        bias_table.reshape(kind_count * heads_n, extent),
        onehot_rel,
        precision=highest,
        preferred_element_type=jnp.float32,
    )
    kind_onehot = (kinds_flat[:, None] == jnp.arange(kind_count, dtype=jnp.int32)[None, :]).astype(
        jnp.float32
    )
    per_window = jnp.dot(
        kind_onehot,
        spread.reshape(kind_count, heads_n * positions * positions),
        precision=highest,
        preferred_element_type=jnp.float32,
    )
    return (per_window.reshape(-1, heads_n, positions, positions), kind_onehot)


def attend_forward(x_windows, norm_gain, w_qkv, w_proj, bias_win, allowed):
    count, positions, channels = x_windows.shape
    head_size = channels // HEADS
    inv_sqrt = head_size ** (-0.5)
    flat_rows = x_windows.reshape(-1, channels).astype(jnp.float32)
    centre = flat_rows - jnp.mean(flat_rows, axis=-1, keepdims=True)
    inverse = lax.rsqrt(jnp.mean(centre * centre, axis=-1, keepdims=True) + norm_eps)
    unit_rows = centre * inverse
    normed = (unit_rows * norm_gain).astype(jnp.bfloat16)
    qkv_rows = jnp.dot(normed, w_qkv, preferred_element_type=jnp.float32).astype(jnp.bfloat16)
    parts_qkv = qkv_rows.reshape(count, positions, 3, HEADS, head_size)
    queries = parts_qkv[:, :, 0]
    keys_in = parts_qkv[:, :, 1]
    values_in = parts_qkv[:, :, 2]
    scores = (
        jnp.einsum("wihd,wjhd->whij", queries, keys_in, preferred_element_type=jnp.float32)
        * inv_sqrt
        + bias_win
    )
    scores = jnp.where(allowed, scores, masked_score)
    soft_probs = jax.nn.softmax(scores, axis=-1)
    probs_low = soft_probs.astype(jnp.bfloat16)
    mixed_rows = jnp.einsum(
        "whij,wjhd->wihd", probs_low, values_in, preferred_element_type=jnp.float32
    )
    mixed_rows = mixed_rows.astype(jnp.bfloat16).reshape(-1, channels)
    branch = jnp.dot(mixed_rows, w_proj, preferred_element_type=jnp.float32).astype(jnp.bfloat16)
    saved = (
        normed,
        unit_rows,
        inverse,
        queries,
        keys_in,
        values_in,
        soft_probs,
        probs_low,
        mixed_rows,
    )
    return (saved, branch)


def attend_backward(
    saved, g_windows, keep_win, w_qkv, w_proj, norm_gain, kind_onehot, onehot_rel, table_dims
):
    normed, unit_rows, inverse, queries, keys_in, values_in, soft_probs, probs_low, mixed_rows = (
        saved
    )
    count, heads_n, positions = (soft_probs.shape[0], soft_probs.shape[1], soft_probs.shape[2])
    channels = normed.shape[1]
    head_size = channels // heads_n
    inv_sqrt = head_size ** (-0.5)
    flat_g = g_windows.reshape(-1, channels)
    keep_rows = keep_win.reshape(-1, 1)
    keep_low = keep_rows.astype(jnp.bfloat16)
    grad_proj = jnp.einsum(
        "nc,nd->cd", mixed_rows * keep_low, flat_g, preferred_element_type=jnp.float32
    )
    d_mixed = jnp.einsum("nd,cd->nc", flat_g, w_proj, preferred_element_type=jnp.float32).astype(
        jnp.bfloat16
    )
    d_mixed = d_mixed.reshape(count, positions, heads_n, head_size)
    d_probs = jnp.einsum("wihd,wjhd->whij", d_mixed, values_in, preferred_element_type=jnp.float32)
    d_values = jnp.einsum(
        "whij,wihd->wjhd", probs_low, d_mixed, preferred_element_type=jnp.float32
    ).astype(jnp.bfloat16)
    d_scores = soft_probs * (d_probs - jnp.sum(soft_probs * d_probs, axis=-1, keepdims=True))
    d_scores_low = d_scores.astype(jnp.bfloat16)
    d_queries = (
        jnp.einsum("whij,wjhd->wihd", d_scores_low, keys_in, preferred_element_type=jnp.float32)
        * inv_sqrt
    ).astype(jnp.bfloat16)
    d_keys = (
        jnp.einsum("whij,wihd->wjhd", d_scores_low, queries, preferred_element_type=jnp.float32)
        * inv_sqrt
    ).astype(jnp.bfloat16)
    d_qkv = jnp.stack([d_queries, d_keys, d_values], axis=2).reshape(-1, 3 * channels)
    grad_qkv = jnp.einsum("nc,nd->cd", normed * keep_low, d_qkv, preferred_element_type=jnp.float32)
    d_normed = jnp.einsum("nd,cd->nc", d_qkv, w_qkv, preferred_element_type=jnp.float32)
    grad_gain = jnp.sum(d_normed * unit_rows * keep_rows, axis=0)
    d_unit = d_normed * norm_gain
    d_path = inverse * (
        d_unit
        - jnp.mean(d_unit, axis=-1, keepdims=True)
        - unit_rows * jnp.mean(d_unit * unit_rows, axis=-1, keepdims=True)
    )
    d_path = d_path.astype(jnp.bfloat16)
    query_keep = keep_win.reshape(count, 1, positions, 1)
    by_kind = jnp.einsum(
        "wk,wx->kx",
        kind_onehot,
        (d_scores * query_keep).reshape(count, -1),
        precision=highest,
        preferred_element_type=jnp.float32,
    )
    grad_table = jnp.dot(
        by_kind.reshape(-1, positions * positions),
        onehot_rel,
        precision=highest,
        preferred_element_type=jnp.float32,
    )
    return (d_path, (grad_qkv, grad_proj, grad_table.reshape(table_dims), grad_gain))


def shifted_pair(source, half_lat, half_lon):
    upper = shifted(source[:half_lat], "lat", -1)
    stacked = jnp.concatenate([source[half_lat:], upper], axis=0)
    right_side = shifted(stacked[:, :half_lon], "lon", -1)
    return jnp.concatenate([stacked[:, half_lon:], right_side], axis=1)


def unshift_pair(block, half_lat, half_lon):
    trailing = shifted(block[:, -half_lon:], "lon", 1)
    placed = jnp.concatenate([trailing, block[:, :-half_lon]], axis=1)
    lower = shifted(placed[-half_lat:], "lat", 1)
    return jnp.concatenate([lower, placed[:-half_lat]], axis=0)


def clip_rms(gradient):
    return gradient * jnp.minimum(
        1.0, clip_level * lax.rsqrt(jnp.mean(gradient * gradient) + clip_eps)
    )


def on_device(state_grid, norm_gain, w_qkv, w_proj, bias_table, window_kind, cotangent):
    rows_dev, cols_dev, channels = state_grid.shape
    half_lat = WIN_LAT // 2
    half_lon = WIN_LON // 2
    positions = WIN_LAT * WIN_LON
    lat_index = lax.axis_index("lat")
    lon_index = lax.axis_index("lon")
    rows_all = rows_dev * lax.axis_size("lat")
    onehot_rel = relation_onehot(WIN_LAT, WIN_LON)
    band_start = lat_index * (rows_dev // WIN_LAT)
    sector_start = lon_index * (cols_dev // WIN_LON)
    first_row = lat_index * rows_dev + half_lat
    types_block = lax.dynamic_slice(
        window_kind, (band_start, sector_start), (rows_dev // WIN_LAT, cols_dev // WIN_LON)
    )
    keep_grid = jnp.ones((rows_dev, cols_dev), jnp.float32)
    joint = jnp.concatenate([state_grid, cotangent], axis=2)
    block_joint = shifted_pair(joint, half_lat, half_lon)
    block_x = block_joint[:, :, :channels]
    block_g = block_joint[:, :, channels:]
    block_rows, block_cols = (block_x.shape[0], block_x.shape[1])
    row_ids = (first_row + jnp.arange(block_rows, dtype=jnp.int32)) % rows_all
    labels = (row_ids + half_lat) // WIN_LAT
    label_grid = jnp.broadcast_to(labels[:, None, None], (block_rows, block_cols, 1))
    label_win = to_windows(label_grid, WIN_LAT, WIN_LON)[:, :, 0]
    allowed = (label_win[:, :, None] == label_win[:, None, :])[:, None]
    keep_win = to_windows(keep_grid[:, :, None], WIN_LAT, WIN_LON)[:, :, 0]
    bias_win, kind_onehot = window_bias(bias_table, types_block.reshape(-1), onehot_rel, positions)
    saved, branch = attend_forward(
        to_windows(block_x, WIN_LAT, WIN_LON), norm_gain, w_qkv, w_proj, bias_win, allowed
    )
    branch_grid = from_windows(
        branch.reshape(-1, positions, channels), block_rows, block_cols, WIN_LAT, WIN_LON
    )
    g_windows = to_windows(block_g, WIN_LAT, WIN_LON)
    d_path, grads = attend_backward(
        saved,
        g_windows,
        keep_win,
        w_qkv,
        w_proj,
        norm_gain,
        kind_onehot,
        onehot_rel,
        bias_table.shape,
    )
    path_grid = from_windows(
        d_path.reshape(-1, positions, channels), block_rows, block_cols, WIN_LAT, WIN_LON
    )
    both_own = unshift_pair(jnp.concatenate([branch_grid, path_grid], axis=2), half_lat, half_lon)
    branch_own = both_own[:, :, :channels]
    path_own = both_own[:, :, channels:]
    out_field = (state_grid.astype(jnp.float32) + branch_own.astype(jnp.float32)).astype(
        jnp.bfloat16
    )
    d_field = (cotangent.astype(jnp.float32) + path_own.astype(jnp.float32)).astype(jnp.bfloat16)
    grad_qkv, grad_proj, grad_table, grad_gain = grads
    summed = packed_total((grad_qkv, grad_proj, grad_table, grad_gain), ("lat", "lon"))
    qkv_grad = clip_rms(summed[0])
    proj_grad = clip_rms(summed[1])
    table_grad = clip_rms(summed[2])
    gain_grad = clip_rms(summed[3])
    return (out_field, d_field, qkv_grad, proj_grad, table_grad, gain_grad)


def solution(mesh):
    in_specs = (P("lat", "lon", None), P(), P(), P(), P(), P(), P("lat", "lon", None))
    out_specs = (P("lat", "lon", None), P("lat", "lon", None), P(), P(), P(), P())
    return jax.shard_map(
        on_device, mesh=mesh, in_specs=in_specs, out_specs=out_specs, check_vma=False
    )
```

profile of v0, /device:TPU:1, one launch (start us, length us, event | category | flops | bytes accessed | tf_op | source)
XLA Modules:
  0.0 382.0 jit_solution(4927379221810846586)
XLA Ops:
  7.2 2.0 fusion.26
  9.2 12.5 %collective-permute-start = (bf16[3,84,384]{2,1,0:T(8,128)(2,1)}, bf16[3,84,384]{2,1,0:T(8,128)(2,1)S(1)}, u32[]{:S(2)}, u32[]{:S(2)}) collective-permute-start(bf16[3,84,384]{2,1,0:T(8,128)(2,1)} %get-tuple-element.25), channel_id=1, source_target_pairs={{0,480},{32,0},{64,32},{96,64},{128,96},{160,128},{192,160},{224,1... | collective-permute-start | bytes 580616 | tf_op jit(solution)/shard_map/ppermute | solution.py:21
  22.9 2.6 convolution_bitcast_fusion
  26.3 2.7 dot_general.59
  29.7 2.8 fusion.4
  32.6 1.6 copy.61
  34.3 2.9 collective-permute-start.1
  37.3 2.6 collective-permute-done.1
  42.4 1.1 reshape.243
  45.0 1.0 reshape.237
  48.3 2.3 fusion.38
  50.6 2.3 fusion.11
  52.9 2.3 fusion.10
  55.2 1.7 multiply_reduce_fusion
  57.9 1.3 fusion.12
  59.2 1.1 fusion.13
  60.7 1.0 copy.75
  61.9 1.2 copy.63
  64.0 1.1 reshape.248
  66.0 1.4 reshape.249
  70.6 2.1 collective-permute-start.2
  72.7 1.9 fusion.1
  74.6 2.4 collective-permute-done.2
  77.2 1.9 collective-permute-start.3
  79.9 5.7 %concatenate.27 = f32[159792]{0:T(1024)} concatenate(f32[110592]{0:T(1024)S(1)} %reshape.246, f32[36864]{0:T(1024)S(1)} %reshape.247, f32[12144]{0:T(1024)S(1)} %reshape_reshape.16, f32[192]{0:T(256)S(1)} %get-tuple-element.18), dimensions={0} | concatenate | bytes 1278336 | tf_op jit(solution)/shard_map/concatenate | solution.py:28
  86.8 272.9 %all-reduce.2.cloned.1.call-done = f32[159792]{0:T(1024)} async-done(((f32[159792]{0:T(1024)}), f32[159792]{0:T(1024)}) %all-reduce.2.cloned.1.call-update) | async-done | bytes 639184 | tf_op jit(solution)/shard_map/psum | solution.py:28
  359.7 1.4 multiply_reduce_fusion.8
  361.7 1.4 multiply_reduce_fusion.7
  363.9 1.6 multiply_reduce_fusion.6
  366.1 1.7 multiply_reduce_fusion.2
  370.1 1.0 slice_multiply_fusion
  373.8 1.3 slice_multiply_fusion.3
  (112 shorter events, 21.7 us)
Async XLA Ops:
  7.2 37.5 %copy-start = (bf16[192,576]{1,0:T(8,128)(2,1)S(1)}, bf16[192,576]{1,0:T(8,128)(2,1)}, u32[]{:S(2)}) copy-start(bf16[192,576]{1,0:T(8,128)(2,1)} %param.9) | copy-start | bytes 663556
  7.2 352.5 %all-reduce.2.cloned.1.call-start = ((), (), s32[]{:S(2)}) async-start(), calls=%async_computation | async-start | bytes 1286144 | tf_op jit(solution)/shard_map/psum | solution.py:28
  9.2 25.1 %collective-permute-start = (bf16[3,84,384]{2,1,0:T(8,128)(2,1)}, bf16[3,84,384]{2,1,0:T(8,128)(2,1)S(1)}, u32[]{:S(2)}, u32[]{:S(2)}) collective-permute-start(bf16[3,84,384]{2,1,0:T(8,128)(2,1)} %get-tuple-element.25), channel_id=1, source_target_pairs={{0,480},{32,0},{64,32},{96,64},{128,96},{160,128},{192,160},{224,1... | collective-permute-start | bytes 580616 | tf_op jit(solution)/shard_map/ppermute | solution.py:21
  34.3 5.6 %collective-permute-start.1 = (bf16[6,6,384]{2,1,0:T(8,128)(2,1)S(1)}, bf16[6,6,384]{2,1,0:T(8,128)(2,1)S(1)}, u32[]{:S(2)}, u32[]{:S(2)}) collective-permute-start(bf16[6,6,384]{2,1,0:T(8,128)(2,1)S(1)} %pad_maximum_fusion.6), channel_id=1, source_target_pairs={{0,31},{1,0},{2,1},{3,2},{4,3},{5,4},{6,5},{7,6},{8,7},{9,8},{10,9... | collective-permute-start | bytes 82952 | tf_op jit(solution)/shard_map/ppermute | solution.py:21
  40.1 0.8 copy-start.18
  40.7 1.5 copy-start.15
  42.2 1.4 copy-start.8
  43.9 0.7 copy-start.2
  46.0 1.6 copy-start.1
  46.9 0.7 copy-start.4
  46.9 1.4 copy-start.6
  56.9 1.0 copy-start.7
  57.9 1.3 copy-start.5
  60.7 2.6 copy-start.16
  65.2 2.2 copy-start.10
  65.9 1.4 copy-start.11
  65.9 1.4 copy-start.17
  67.6 1.5 copy-start.3
  70.2 2.6 copy-start.14
  70.6 8.5 %copy-start.9 = (bf16[504,192]{1,0:T(8,128)(2,1)S(1)}, bf16[504,192]{1,0:T(8,128)(2,1)}, u32[]{:S(2)}) copy-start(bf16[504,192]{1,0:T(8,128)(2,1)} %copy-done.8) | copy-start | bytes 580612
  70.6 6.3 %collective-permute-start.2 = (bf16[6,6,384]{2,1,0:T(8,128)(2,1)S(1)}, bf16[6,6,384]{2,1,0:T(8,128)(2,1)S(1)}, u32[]{:S(2)}, u32[]{:S(2)}) collective-permute-start(bf16[6,6,384]{2,1,0:T(8,128)(2,1)S(1)} %pad_maximum_fusion.5), channel_id=1, source_target_pairs={{0,1},{1,2},{2,3},{3,4},{4,5},{5,6},{6,7},{7,8},{8,9},{9,10},{10,1... | collective-permute-start | bytes 82952 | tf_op jit(solution)/shard_map/ppermute | solution.py:21
  77.2 8.6 %collective-permute-start.3 = (bf16[3,84,384]{2,1,0:T(8,128)(2,1)S(1)}, bf16[3,84,384]{2,1,0:T(8,128)(2,1)S(1)}, u32[]{:S(2)}, u32[]{:S(2)}) collective-permute-start(bf16[3,84,384]{2,1,0:T(8,128)(2,1)S(1)} %get-tuple-element.29), channel_id=1, source_target_pairs={{0,32},{32,64},{64,96},{96,128},{128,160},{160,192},{192,224},{224... | collective-permute-start | bytes 580616 | tf_op jit(solution)/shard_map/ppermute | solution.py:21
  79.5 6.3 %copy-start.12 = (bf16[6,84,192]{2,1,0:T(8,128)(2,1)S(1)}, bf16[6,84,192]{2,1,0:T(8,128)(2,1)}, u32[]{:S(2)}) copy-start(bf16[6,84,192]{2,1,0:T(8,128)(2,1)} %param.13) | copy-start | bytes 580612
  79.5 6.3 %copy-start.13 = (bf16[6,84,192]{2,1,0:T(8,128)(2,1)S(1)}, bf16[6,84,192]{2,1,0:T(8,128)(2,1)}, u32[]{:S(2)}) copy-start(bf16[6,84,192]{2,1,0:T(8,128)(2,1)} %param.7) | copy-start | bytes 580612
Sparse Core Ops, SparseCore 0:
  85.8 273.8 all-reduce.1
where the time goes:
time: 384 us; the launch traced here: 382 us
  waiting for transfers between devices  278 us (72%)
  local copies, waits for them, and re-layouts  29.3 us (8%)
  starting transfers between devices  19.4 us (5%)
  matrix products  19.3 us (5%)
  other arithmetic  18.5 us (5%)
  between operations  17.5 us (5%)
    psum x1, waiting for transfers between devices, packed_total(): so_far = lax.psum(jnp.concatenate([a.ravel() for a in arrays]), axis)  273 us
    ppermute x4, starting transfers between devices, shifted(): return lax.ppermute(value, axis, pairs)  19.3 us
  transfers between devices with their start and end apart: 5, of which 4 were waited for; matrix products, arithmetic and copies ran while one was open for 6% of the time, Pallas kernels for 0%

commit v1 on v0

v1 whole, which is shorter than its diff:
```python
import functools
import jax
import jax.numpy as jnp
from jax import lax
from jax.experimental import pallas as pl
from jax.experimental.pallas import tpu as pltpu
from jax.sharding import PartitionSpec as P

HEADS = 6
WIN_LAT = 6
WIN_LON = 12
HEAD = 32
D = 192
PITCH = 16
TOK = WIN_LAT * PITCH
LANES = 128
SPAN = 256
norm_eps = 1e-05
clip_eps = 1e-06
masked = -1e30
highest = lax.Precision.HIGHEST
f32 = jnp.float32
bf16 = jnp.bfloat16

NT = (((1,), (1,)), ((), ()))
TN = (((0,), (0,)), ((), ()))


def nt(a, b, **kw):
    return lax.dot_general(a, b, NT, preferred_element_type=f32, **kw)


def tn(a, b, **kw):
    return lax.dot_general(a, b, TN, preferred_element_type=f32, **kw)


def nn(a, b, **kw):
    return jnp.dot(a, b, preferred_element_type=f32, **kw)


def iota(shape, dim):
    return lax.broadcasted_iota(jnp.int32, shape, dim)


def base_pattern():
    p = iota((SPAN, SPAN), 0)
    lane = iota((SPAN, SPAN), 1)
    d = lane // PITCH
    c = lane % PITCH
    hit = (p == (2 * WIN_LAT - 2 - d) * (2 * WIN_LON - 1) - c + WIN_LON - 1) & (c < WIN_LON) & (d < 2 * WIN_LAT - 1)
    return hit.astype(f32)


def kernel(windows, meta_ref, s_ref, g_ref, up_ref, rt_ref, cr_ref, gain_ref, wqkv_ref, wproj_ref, table_ref,
           both_ref, gq_ref, gp_ref, gt_ref, gg_ref,
           xs, gs, tilt, span, bias, un, nm, inv, q_s, k_s, v_s, dm_s, mix, dq_s, dk_s, dv_s, fold):
    half_lat = WIN_LAT // 2
    half_lon = WIN_LON // 2
    own = windows * WIN_LON - half_lon
    kinds = table_ref.shape[0] // HEADS

    for c in range(PITCH):
        moved = table_ref[...] if c == 0 else pltpu.roll(table_ref[...], SPAN - c, axis=1)
        for half in range(2):
            tilt[half, pl.ds(c, kinds * HEADS, stride=PITCH), :] = moved[:, half * LANES:(half + 1) * LANES]
    pattern = base_pattern()
    span[...] = nn(jnp.concatenate([tilt[0], tilt[1]], axis=1), pattern, precision=highest)
    slot = iota((PITCH, LANES), 1)
    open_slot = (slot % PITCH < WIN_LON) & (slot < TOK)
    split = meta_ref[windows] > 0

    def spread(n, carry):
        wide = span[pl.ds(pl.multiple_of(n * PITCH, PITCH), PITCH), :]
        for r in range(WIN_LAT):
            off = (WIN_LAT - 1 - r) * PITCH
            part = wide if off == 0 else pltpu.roll(wide, SPAN - off, axis=1)
            other = (slot < half_lat * PITCH) if r >= half_lat else (slot >= half_lat * PITCH)
            ok = open_slot & jnp.logical_not(split & other)
            bias[n // HEADS, pl.ds(pl.multiple_of((n % HEADS) * TOK + r * PITCH, PITCH), PITCH), :] = jnp.where(ok, part[:, :LANES], masked)
        return carry

    lax.fori_loop(0, kinds * HEADS, spread, 0)
    fold[...] = jnp.zeros_like(fold)

    xs[...] = jnp.zeros_like(xs)
    gs[...] = jnp.zeros_like(gs)
    for w in range(windows):
        for r in range(WIN_LAT):
            at = w * TOK + r * PITCH
            start = half_lon + w * WIN_LON
            inside = WIN_LON if w < windows - 1 else half_lon
            for dst, src, lo in ((xs, s_ref, 0), (gs, g_ref, D)):
                if r < half_lat:
                    dst[at:at + inside, :] = src[r + half_lat, start:start + inside, :]
                    if inside < WIN_LON:
                        dst[at + inside:at + WIN_LON, :] = rt_ref[r, :, lo:lo + D]
                else:
                    dst[at:at + inside, :] = up_ref[r - half_lat, start:start + inside, lo:lo + D]
                    if inside < WIN_LON:
                        dst[at + inside:at + WIN_LON, :] = cr_ref[r - half_lat, :, lo:lo + D]

    gain = gain_ref[...]
    x = xs[...].astype(f32)
    centre = x - jnp.mean(x, axis=-1, keepdims=True)
    inverse = lax.rsqrt(jnp.mean(centre * centre, axis=-1, keepdims=True) + norm_eps)
    unit = centre * inverse
    un[...] = unit
    inv[...] = inverse
    normed = (unit * gain).astype(bf16)
    nm[...] = normed
    wq, wk, wv = (wqkv_ref[:, i * D:(i + 1) * D] for i in range(3))
    q_s[...] = nn(normed, wq).astype(bf16)
    k_s[...] = nn(normed, wk).astype(bf16)
    v_s[...] = nn(normed, wv).astype(bf16)
    dm_s[...] = nt(gs[...], wproj_ref[...]).astype(bf16)

    scale = HEAD ** (-0.5)
    head_of = iota((TOK, D), 1) // HEAD
    pads = jnp.zeros((LANES - TOK, D), bf16)

    def by_head(a):
        zero = jnp.zeros_like(a)
        return [jnp.where(head_of == h, a, zero) for h in range(HEADS)]

    def window(w, carry):
        rows = pl.ds(pl.multiple_of(w * TOK, TOK), TOK)
        kind = meta_ref[w]
        q, k, v, dm = q_s[rows, :], k_s[rows, :], v_s[rows, :], dm_s[rows, :]
        q_heads = jnp.concatenate(by_head(q), axis=0)
        dm_heads = jnp.concatenate(by_head(dm), axis=0)
        k_pad = jnp.concatenate([k, pads], axis=0)
        v_pad = jnp.concatenate([v, pads], axis=0)
        scores = nt(q_heads, k_pad) * scale + bias[kind]
        top = jnp.max(scores, axis=-1, keepdims=True)
        raised = jnp.exp(scores - top)
        probs = raised * (1.0 / jnp.sum(raised, axis=-1, keepdims=True))
        probs_low = probs.astype(bf16)
        d_probs = nt(dm_heads, v_pad)
        d_scores = probs * (d_probs - jnp.sum(probs * d_probs, axis=-1, keepdims=True))
        low = d_scores.astype(bf16)
        side = lambda a: jnp.concatenate([a[h * TOK:(h + 1) * TOK] for h in range(HEADS)], axis=1)
        tall = lambda a: jnp.concatenate([b for part in by_head(a) for b in (part, pads)], axis=0)
        mix[rows, :] = nn(side(probs_low), tall(v)).astype(bf16)
        dq_s[rows, :] = (nn(side(low), tall(k)) * scale).astype(bf16)
        dv_s[rows, :] = tn(probs_low, dm_heads)[:TOK].astype(bf16)
        dk_s[rows, :] = (tn(low, q_heads) * scale)[:TOK].astype(bf16)
        lane = iota((PITCH, SPAN), 1)
        for h in range(HEADS):
            total = None
            for r in range(WIN_LAT):
                off = (WIN_LAT - 1 - r) * PITCH
                part = d_scores[h * TOK + r * PITCH:h * TOK + (r + 1) * PITCH]
                part = jnp.concatenate([part, jnp.zeros_like(part)], axis=1)
                if off:
                    part = pltpu.roll(part, off, axis=1)
                total = part if total is None else total + part
            fold[kind, h * PITCH:(h + 1) * PITCH, :] += total
        return carry

    lax.fori_loop(0, windows, window, 0)

    branch = nn(mix[...], wproj_ref[...]).astype(bf16)
    gp_ref[...] = tn(mix[...], gs[...])
    d_normed = nt(dq_s[...], wq) + nt(dk_s[...], wk) + nt(dv_s[...], wv)
    for i, d in enumerate((dq_s, dk_s, dv_s)):
        gq_ref[:, i * D:(i + 1) * D] = tn(nm[...], d[...])
    unit = un[...]
    gg_ref[...] = jnp.sum(d_normed * unit, axis=0, keepdims=True)
    d_unit = d_normed * gain
    path = inv[...] * (d_unit - jnp.mean(d_unit, axis=-1, keepdims=True) - unit * jnp.mean(d_unit * unit, axis=-1, keepdims=True))
    path = path.astype(bf16)
    for w in range(windows):
        for r in range(WIN_LAT):
            at = w * TOK + r * PITCH
            both_ref[r, w * WIN_LON:(w + 1) * WIN_LON, 0:D] = branch[at:at + WIN_LON]
            both_ref[r, w * WIN_LON:(w + 1) * WIN_LON, D:2 * D] = path[at:at + WIN_LON]

    back = nt(fold[...].reshape(kinds * HEADS * PITCH, SPAN), pattern, precision=highest)
    for half in range(2):
        tilt[half] = back[:, half * LANES:(half + 1) * LANES]
    total = None
    for c in range(WIN_LON):
        part = jnp.concatenate([tilt[half, pl.ds(c, kinds * HEADS, stride=PITCH), :] for half in range(2)], axis=1)
        if c:
            part = pltpu.roll(part, c, axis=1)
        total = part if total is None else total + part
    gt_ref[...] = total


def attend(meta, s, g, up, rt, cr, gain, w_qkv, w_proj, table):
    windows = s.shape[1] // WIN_LON
    n = windows * TOK
    vm = pl.BlockSpec(memory_space=pltpu.VMEM)
    kh = table.shape[0]
    return pl.pallas_call(
        functools.partial(kernel, windows),
        out_shape=(
            jax.ShapeDtypeStruct(s.shape[:2] + (2 * D,), bf16),
            jax.ShapeDtypeStruct((D, 3 * D), f32),
            jax.ShapeDtypeStruct((D, D), f32),
            jax.ShapeDtypeStruct((kh, SPAN), f32),
            jax.ShapeDtypeStruct((1, D), f32),
        ),
        in_specs=[pl.BlockSpec(memory_space=pltpu.SMEM)] + [vm] * 9,
        out_specs=(vm,) * 5,
        scratch_shapes=[
            pltpu.VMEM((n, D), bf16), pltpu.VMEM((n, D), bf16),
            pltpu.VMEM((2, kh * PITCH, LANES), f32), pltpu.VMEM((kh * PITCH, SPAN), f32),
            pltpu.VMEM((kh // HEADS, HEADS * TOK, LANES), f32),
            pltpu.VMEM((n, D), f32), pltpu.VMEM((n, D), bf16), pltpu.VMEM((n, 1), f32),
        ] + [pltpu.VMEM((n, D), bf16)] * 8 + [pltpu.VMEM((kh // HEADS, HEADS * PITCH, SPAN), f32)],
        cost_estimate=pl.CostEstimate(flops=2_000_000_000, bytes_accessed=4_000_000, transcendentals=500_000),
        name="attend",
    )(meta, s, g, up, rt, cr, gain, w_qkv, w_proj, table)


def shifted(value, axis, steps):
    count = lax.axis_size(axis)
    return lax.ppermute(value, axis, [(i, (i + steps) % count) for i in range(count)])


def clip_rms(gradient, count):
    return gradient * jnp.minimum(1.0, lax.rsqrt(jnp.sum(gradient * gradient) / count + clip_eps))


ROWS = 1280


def total_of(packed):
    sizes = [lax.axis_size(a) for a in ("lat", "lon")]
    part = packed
    for axis, n in zip(("lat", "lon"), sizes):
        part = part.reshape((n, -1) + part.shape[1:]) if part.shape[0] % n == 0 else part.reshape(n, -1)
        got = lax.all_to_all(part, axis, 0, 0, tiled=True)
        part = jnp.sum(got.astype(f32), axis=0).astype(bf16)
    for axis, n in zip(("lon", "lat"), sizes[::-1]):
        part = lax.all_to_all(jnp.broadcast_to(part[None], (n,) + part.shape), axis, 0, 0, tiled=True)
    return part.reshape(-1)


def on_device(state_grid, norm_gain, w_qkv, w_proj, bias_table, window_kind, cotangent):
    rows_dev, cols_dev, channels = state_grid.shape
    half_lat, half_lon = WIN_LAT // 2, WIN_LON // 2
    lat, lon = lax.axis_index("lat"), lax.axis_index("lon")
    windows = cols_dev // WIN_LON
    joint = jnp.concatenate([state_grid[:half_lat], cotangent[:half_lat]], axis=2)
    up = shifted(joint, "lat", -1)
    side = jnp.concatenate([state_grid[half_lat:, :half_lon], cotangent[half_lat:, :half_lon]], axis=2)
    side = shifted(jnp.concatenate([side, up[:, :half_lon]], axis=0), "lon", -1)
    kinds = lax.dynamic_slice(window_kind, (lat, lon * windows), (1, windows))[0]
    last = (lat == lax.axis_size("lat") - 1).astype(jnp.int32)
    meta = jnp.concatenate([kinds, last[None]])
    kind_count, heads, extent = bias_table.shape
    table = jnp.pad(bias_table.reshape(kind_count * heads, extent), ((0, 0), (0, SPAN - extent)))
    both, gq, gp, gt, gg = attend(
        meta, state_grid, cotangent, up, side[:half_lat], side[half_lat:], norm_gain.reshape(1, -1), w_qkv, w_proj, table
    )
    moved = shifted(both[:, -half_lon:], "lon", 1)
    placed = jnp.concatenate([moved, both[:, :-half_lon]], axis=1)
    lower = shifted(placed[half_lat:], "lat", 1)
    own = jnp.concatenate([lower, placed[:half_lat]], axis=0).astype(f32)
    out_field = (state_grid.astype(f32) + own[:, :, :channels]).astype(bf16)
    d_field = (cotangent.astype(f32) + own[:, :, channels:]).astype(bf16)
    pieces = [gq, gp, gt[:, :extent], gg]
    flat = jnp.concatenate([p.astype(bf16).ravel() for p in pieces])
    flat = jnp.pad(flat, (0, ROWS * LANES - flat.size))
    summed = total_of(flat.reshape(ROWS, LANES))
    outs, at = [], 0
    for p in pieces:
        size = 1
        for n in p.shape:
            size *= n
        outs.append(clip_rms(summed[at:at + size].astype(f32), size))
        at += size
    return (out_field, d_field, outs[0].reshape(w_qkv.shape), outs[1].reshape(w_proj.shape),
            outs[2].reshape(bias_table.shape), outs[3])


def solution(mesh):
    in_specs = (P("lat", "lon", None), P(), P(), P(), P(), P(), P("lat", "lon", None))
    out_specs = (P("lat", "lon", None), P("lat", "lon", None), P(), P(), P(), P())
    return jax.shard_map(on_device, mesh=mesh, in_specs=in_specs, out_specs=out_specs, check_vma=False)
```

time: 384 us -> 130 us (0.34)
  waiting for transfers between devices: 278 us -> 22.6 us
  blocking collectives: 0 us -> 34.4 us
  matrix products: 19.3 us -> 0 us
  local copies, waits for them, and re-layouts: 29.3 us -> 10.9 us
  Pallas kernels: 0 us -> 16.9 us
  between operations: 17.5 us -> 3.74 us
  starting transfers between devices: 19.4 us -> 32.5 us
  other arithmetic: 18.5 us -> 8.14 us
    psum x1 -> x0, waiting for transfers between devices: 273 us -> none  [packed_total(): so_far = lax.psum(jnp.concatenate([a.ravel() for a in arrays]), axis)]
    all_to_all x0 -> x2, blocking collectives: none -> 34.4 us  [total_of(): got = lax.all_to_all(part, axis, 0, 0, tiled=True)]
    dot_general x16 -> x0, matrix products: 19.3 us -> none  [the longest x1 2.81 us: window_bias(): jnp.dot(kind_onehot, spread.reshape(kind_count, heads_n * positions * pos...]
    pallas_call x0 -> x1, Pallas kernels: none -> 16.9 us  [attend(): pl.pallas_call(functools.partial(kernel, windows), out_shape=(jax.ShapeDt...]
    ppermute x4, waiting for transfers between devices: 5.16 us -> 16.4 us  [shifted(): lax.ppermute(value, axis, [(i, (i + steps) % count) for i in range(count)])]
    all_to_all x0 -> x2, starting transfers between devices: none -> 9.61 us  [total_of(): lax.all_to_all(jnp.broadcast_to(part[None], (n,) + part.shape), axis, 0,...]
    all_to_all x0 -> x2, waiting for transfers between devices: none -> 6.19 us  [total_of(): lax.all_to_all(jnp.broadcast_to(part[None], (n,) + part.shape), axis, 0,...]
    reshape x13 -> x5, local copies, waits for them, and re-layouts: 7.04 us -> 1.09 us  [the longest x3 0.6 us: on_device(): flat = jnp.concatenate([p.astype(bf16).ravel() for p in pieces])]
  transfers between devices with their start and end apart: 5 -> 6, of which waited for: 4 -> 4; matrix products, arithmetic and copies ran while one was open for 6% -> 3% of each run, Pallas kernels for 0% -> 0%
where the time goes in v1:
time: 130 us; the launch traced here: 129 us
  blocking collectives  34.4 us (26%)
  starting transfers between devices  32.5 us (25%)
  waiting for transfers between devices  22.6 us (17%)
  Pallas kernels  16.9 us (13%)
  local copies, waits for them, and re-layouts  10.9 us (8%)
  other arithmetic  8.14 us (6%)
  between operations  3.74 us (3%)
    all_to_all x2, blocking collectives, total_of(): got = lax.all_to_all(part, axis, 0, 0, tiled=True)  34.4 us
    ppermute x4, starting transfers between devices, shifted(): lax.ppermute(value, axis, [(i, (i + steps) % count) for i in range(count)])  22.9 us
    pallas_call x1, Pallas kernels, attend(): pl.pallas_call(functools.partial(kernel, windows), out_shape=(jax.ShapeDt...  16.9 us
    ppermute x4, waiting for transfers between devices, shifted(): lax.ppermute(value, axis, [(i, (i + steps) % count) for i in range(count)])  16.4 us
    all_to_all x2, starting transfers between devices, total_of(): lax.all_to_all(jnp.broadcast_to(part[None], (n,) + part.shape), axis, 0,...  9.61 us
    all_to_all x2, waiting for transfers between devices, total_of(): lax.all_to_all(jnp.broadcast_to(part[None], (n,) + part.shape), axis, 0,...  6.19 us
    reduce_sum x4, other arithmetic, clip_rms(): jnp.sum(gradient * gradient) / count + clip_eps  2.63 us
  transfers between devices with their start and end apart: 6, of which 4 were waited for; matrix products, arithmetic and copies ran while one was open for 3% of the time, Pallas kernels for 0%

profile of v1, /device:TPU:1, one launch (start us, length us, event | category | flops | bytes accessed | tf_op | source)
XLA Modules:
  0.0 129.1 jit_solution(5293191108170468731)
XLA Ops:
  0.7 1.0 slice-done
  1.8 12.5 %collective-permute-start = (bf16[3,84,384]{2,1,0:T(8,128)(2,1)S(1)}, bf16[3,84,384]{2,1,0:T(8,128)(2,1)S(1)}, u32[]{:S(2)}, u32[]{:S(2)}) collective-permute-start(bf16[3,84,384]{2,1,0:T(8,128)(2,1)S(1)} %pad_maximum_fusion.1), channel_id=1, source_target_pairs={{0,480},{32,0},{64,32},{96,64},{128,96},{160,128},{192,160},{224,1... | collective-permute-start | bytes 580616 | tf_op jit(solution)/shard_map/ppermute | solution.py:219
  14.5 3.6 %collective-permute-done.up_ref = bf16[3,84,384]{2,1,0:T(8,128)(2,1)S(1)} collective-permute-done((bf16[3,84,384]{2,1,0:T(8,128)(2,1)S(1)}, bf16[3,84,384]{2,1,0:T(8,128)(2,1)S(1)}, u32[]{:S(2)}, u32[]{:S(2)}) %collective-permute-start) | collective-permute-done | bytes 193568 | tf_op jit(solution)/shard_map/ppermute | solution.py:219
  18.1 3.4 %collective-permute-start.1 = (bf16[6,6,384]{2,1,0:T(8,128)(2,1)S(1)}, bf16[6,6,384]{2,1,0:T(8,128)(2,1)S(1)}, u32[]{:S(2)}, u32[]{:S(2)}) collective-permute-start(bf16[6,6,384]{2,1,0:T(8,128)(2,1)S(1)} %pad_maximum_fusion.2), channel_id=1, source_target_pairs={{0,31},{1,0},{2,1},{3,2},{4,3},{5,4},{6,5},{7,6},{8,7},{9,8},{10,9... | collective-permute-start | bytes 82952 | tf_op jit(solution)/shard_map/ppermute | solution.py:219
  21.6 0.7 pad_add_fusion.meta_ref
  22.3 0.6 pad.8.table_ref
  22.9 1.4 %collective-permute-done.1 = bf16[6,6,384]{2,1,0:T(8,128)(2,1)S(1)} collective-permute-done((bf16[6,6,384]{2,1,0:T(8,128)(2,1)S(1)}, bf16[6,6,384]{2,1,0:T(8,128)(2,1)S(1)}, u32[]{:S(2)}, u32[]{:S(2)}) %collective-permute-start.1) | collective-permute-done | bytes 27680 | tf_op jit(solution)/shard_map/ppermute | solution.py:219
  24.9 16.9 %attend.1 = (bf16[6,84,384]{2,1,0:T(8,128)(2,1)}, f32[192,576]{1,0:T(8,128)}, f32[192,192]{1,0:T(8,128)}, f32[48,256]{1,0:T(8,128)}, f32[1,192]{1,0:T(1,128)}) custom-call(s32[8]{0:T(128)} %pad_add_fusion.meta_ref, bf16[6,84,192]{2,1,0:T(8,128)(2,1)} %s_ref.1, bf16[6,84,192]{2,1,0:T(8,128)(2,1)} %g_ref.1, bf16[3,84,384]{2,1,0:T(8,128)(2,1)} %copy-done.9, ...), custom_call_target="tpu_custom_call" | custom-call | flops 2000000000 | bytes 4000000 | tf_op jit(solution)/shard_map/attend/pallas_call | solution.py:195
  41.8 1.1 convert_element_type.57
  43.2 0.7 copy-done.10
  44.3 1.7 %concatenate.27 = bf16[159792]{0:T(1024)(128)(2,1)S(1)} concatenate(bf16[110592]{0:T(1024)(128)(2,1)S(1)} %reshape.62, bf16[36864]{0:T(1024)(128)(2,1)S(1)} %reshape.63, bf16[12144]{0:T(1024)(128)(2,1)S(1)} %reshape.64, bf16[192]{0:T(256)(128)(2,1)S(1)} %convert_reduce_fusion), dimensions={0} | concatenate | bytes 639168 | tf_op jit(solution)/shard_map/concatenate | solution.py:265
  46.0 13.5 %all_to_all.26 = bf16[16,80,128]{2,1,0:T(8,128)(2,1)S(1)} all-to-all(bf16[16,80,128]{2,1,0:T(8,128)(2,1)S(1)} %bitcast.8), channel_id=1, replica_groups=mesh['lat'=16,'lon'=32] {'lat'}, dimensions={0} | all-to-all | bytes 655360 | tf_op jit(solution)/shard_map/all_to_all | solution.py:234
  60.1 0.8 reduce.5
  61.0 20.9 %all_to_all.27 = bf16[32,2,160]{2,1,0:T(2,128)(2,1)S(1)} all-to-all(bf16[32,2,160]{2,1,0:T(2,128)(2,1)S(1)} %reshape.69), channel_id=1, replica_groups=mesh['lat'=16,'lon'=32] {'lon'}, dimensions={0} | all-to-all | bytes 40960 | tf_op jit(solution)/shard_map/all_to_all | solution.py:234
  82.1 0.8 reduce.6
  82.9 0.7 reshape.71
  83.6 3.9 %all-to-all-start.2 = ((bf16[32,2,160]{2,1,0:T(2,128)(2,1)}), bf16[32,2,160]{2,1,0:T(2,128)(2,1)S(1)}, u32[]{:S(2)}, u32[]{:S(2)}) async-start(bf16[32,2,160]{2,1,0:T(2,128)(2,1)} %reshape.71), calls=%async_computation.2 | async-start | bytes 65536 | tf_op jit(solution)/shard_map/all_to_all | solution.py:237
  87.5 3.5 %collective-permute-start.2 = (bf16[6,6,384]{2,1,0:T(8,128)(2,1)S(1)}, bf16[6,6,384]{2,1,0:T(8,128)(2,1)S(1)}, u32[]{:S(2)}, u32[]{:S(2)}) collective-permute-start(bf16[6,6,384]{2,1,0:T(8,128)(2,1)S(1)} %slice.62), channel_id=1, source_target_pairs={{0,1},{1,2},{2,3},{3,4},{4,5},{5,6},{6,7},{7,8},{8,9},{9,10},{10,1... | collective-permute-start | bytes 82952 | tf_op jit(solution)/shard_map/ppermute | solution.py:219
  91.1 6.2 %all-to-all-done.2 = bf16[32,2,160]{2,1,0:T(2,128)(2,1)S(1)} async-done(((bf16[32,2,160]{2,1,0:T(2,128)(2,1)}), bf16[32,2,160]{2,1,0:T(2,128)(2,1)S(1)}, u32[]{:S(2)}, u32[]{:S(2)}) %all-to-all-start.2) | async-done | bytes 20512 | tf_op jit(solution)/shard_map/all_to_all | solution.py:237
  97.4 0.8 broadcast_in_dim.24
  98.2 5.7 %all-to-all-start.3 = ((bf16[16,32,320]{2,1,0:T(8,128)(2,1)}), bf16[16,32,320]{2,1,0:T(8,128)(2,1)S(1)}, u32[]{:S(2)}, u32[]{:S(2)}) async-start(bf16[16,32,320]{2,1,0:T(8,128)(2,1)} %broadcast_in_dim.24), calls=%async_computation.3 | async-start | bytes 786432 | tf_op jit(solution)/shard_map/all_to_all | solution.py:237
  104.0 3.4 %collective-permute-start.3 = (bf16[3,84,384]{2,1,0:T(8,128)(2,1)S(1)}, bf16[3,84,384]{2,1,0:T(8,128)(2,1)S(1)}, u32[]{:S(2)}, u32[]{:S(2)}) collective-permute-start(bf16[3,84,384]{2,1,0:T(8,128)(2,1)S(1)} %fusion.5), channel_id=1, source_target_pairs={{0,32},{32,64},{64,96},{96,128},{128,160},{160,192},{192,224},{224... | collective-permute-start | bytes 580616 | tf_op jit(solution)/shard_map/ppermute | solution.py:219
  107.5 11.4 %collective-permute-done.3 = bf16[3,84,384]{2,1,0:T(8,128)(2,1)S(1)} collective-permute-done((bf16[3,84,384]{2,1,0:T(8,128)(2,1)S(1)}, bf16[3,84,384]{2,1,0:T(8,128)(2,1)S(1)}, u32[]{:S(2)}, u32[]{:S(2)}) %collective-permute-start.3) | collective-permute-done | bytes 193568 | tf_op jit(solution)/shard_map/ppermute | solution.py:219
  119.0 1.1 fusion
  120.5 0.7 fusion.8
  121.2 0.6 fusion.7
  121.8 0.6 fusion.6
  122.4 0.7 fusion.2
  125.9 0.6 convert_multiply_fusion.6
  126.7 0.6 copy.23
  127.4 0.8 mul.59
  128.2 0.9 mul.55
  (60 shorter events, 3.6 us)
Async XLA Ops:
  0.6 13.8 %copy-start = (s32[16,224]{1,0:T(8,128)S(1)}, s32[16,224]{1,0:T(8,128)}, u32[]{:S(2)}) copy-start(s32[16,224]{1,0:T(8,128)} %param.12) | copy-start | bytes 43012
  0.6 13.7 %copy-start.3 = (bf16[6,84,192]{2,1,0:T(8,128)(2,1)S(1)}, bf16[6,84,192]{2,1,0:T(8,128)(2,1)}, u32[]{:S(2)}) copy-start(bf16[6,84,192]{2,1,0:T(8,128)(2,1)} %g_ref.1) | copy-start | bytes 580612
  0.7 1.0 slice-start
  0.7 1.1 slice-start.1
  1.7 12.6 %copy-start.1 = (bf16[6,84,192]{2,1,0:T(8,128)(2,1)S(1)}, bf16[6,84,192]{2,1,0:T(8,128)(2,1)}, u32[]{:S(2)}) copy-start(bf16[6,84,192]{2,1,0:T(8,128)(2,1)} %s_ref.1) | copy-start | bytes 580612
  1.8 16.2 %collective-permute-start = (bf16[3,84,384]{2,1,0:T(8,128)(2,1)S(1)}, bf16[3,84,384]{2,1,0:T(8,128)(2,1)S(1)}, u32[]{:S(2)}, u32[]{:S(2)}) collective-permute-start(bf16[3,84,384]{2,1,0:T(8,128)(2,1)S(1)} %pad_maximum_fusion.1), channel_id=1, source_target_pairs={{0,480},{32,0},{64,32},{96,64},{128,96},{160,128},{192,160},{224,1... | collective-permute-start | bytes 580616 | tf_op jit(solution)/shard_map/ppermute | solution.py:219
  18.0 4.9 %copy-start.9 = (bf16[3,84,384]{2,1,0:T(8,128)(2,1)}, bf16[3,84,384]{2,1,0:T(8,128)(2,1)S(1)}, u32[]{:S(2)}) copy-start(bf16[3,84,384]{2,1,0:T(8,128)(2,1)S(1)} %collective-permute-done.up_ref) | copy-start | bytes 580612
  18.1 4.2 %copy-start.7 = (f32[8,6,253]{2,0,1:T(8,128)S(1)}, f32[8,6,253]{2,0,1:T(8,128)}, u32[]{:S(2)}) copy-start(f32[8,6,253]{2,0,1:T(8,128)} %param.11) | copy-start | bytes 145732
  18.1 6.2 %collective-permute-start.1 = (bf16[6,6,384]{2,1,0:T(8,128)(2,1)S(1)}, bf16[6,6,384]{2,1,0:T(8,128)(2,1)S(1)}, u32[]{:S(2)}, u32[]{:S(2)}) collective-permute-start(bf16[6,6,384]{2,1,0:T(8,128)(2,1)S(1)} %pad_maximum_fusion.2), channel_id=1, source_target_pairs={{0,31},{1,0},{2,1},{3,2},{4,3},{5,4},{6,5},{7,6},{8,7},{9,8},{10,9... | collective-permute-start | bytes 82952 | tf_op jit(solution)/shard_map/ppermute | solution.py:219
  42.9 1.0 copy-start.8
  42.9 1.2 copy-start.6
  43.2 0.7 copy-start.10
  59.5 28.0 %copy-start.5 = (bf16[6,84,384]{2,1,0:T(8,128)(2,1)S(1)}, bf16[6,84,384]{2,1,0:T(8,128)(2,1)}, u32[]{:S(2)}) copy-start(bf16[6,84,384]{2,1,0:T(8,128)(2,1)} %get-tuple-element.11) | copy-start | bytes 1161220
  83.6 13.7 %all-to-all-start.2 = ((bf16[32,2,160]{2,1,0:T(2,128)(2,1)}), bf16[32,2,160]{2,1,0:T(2,128)(2,1)S(1)}, u32[]{:S(2)}, u32[]{:S(2)}) async-start(bf16[32,2,160]{2,1,0:T(2,128)(2,1)} %reshape.71), calls=%async_computation.2 | async-start | bytes 65536 | tf_op jit(solution)/shard_map/all_to_all | solution.py:237
  87.5 16.4 %collective-permute-start.2 = (bf16[6,6,384]{2,1,0:T(8,128)(2,1)S(1)}, bf16[6,6,384]{2,1,0:T(8,128)(2,1)S(1)}, u32[]{:S(2)}, u32[]{:S(2)}) collective-permute-start(bf16[6,6,384]{2,1,0:T(8,128)(2,1)S(1)} %slice.62), channel_id=1, source_target_pairs={{0,1},{1,2},{2,3},{3,4},{4,5},{5,6},{6,7},{7,8},{8,9},{9,10},{10,1... | collective-permute-start | bytes 82952 | tf_op jit(solution)/shard_map/ppermute | solution.py:219
  98.2 21.8 %all-to-all-start.3 = ((bf16[16,32,320]{2,1,0:T(8,128)(2,1)}), bf16[16,32,320]{2,1,0:T(8,128)(2,1)S(1)}, u32[]{:S(2)}, u32[]{:S(2)}) async-start(bf16[16,32,320]{2,1,0:T(8,128)(2,1)} %broadcast_in_dim.24), calls=%async_computation.3 | async-start | bytes 786432 | tf_op jit(solution)/shard_map/all_to_all | solution.py:237
  104.0 14.9 %copy-start.2 = (bf16[6,84,192]{2,1,0:T(8,128)(2,1)S(1)}, bf16[6,84,192]{2,1,0:T(8,128)(2,1)}, u32[]{:S(2)}) copy-start(bf16[6,84,192]{2,1,0:T(8,128)(2,1)} %s_ref.1) | copy-start | bytes 580612
  104.0 14.9 %copy-start.4 = (bf16[6,84,192]{2,1,0:T(8,128)(2,1)S(1)}, bf16[6,84,192]{2,1,0:T(8,128)(2,1)}, u32[]{:S(2)}) copy-start(bf16[6,84,192]{2,1,0:T(8,128)(2,1)} %g_ref.1) | copy-start | bytes 580612
  104.0 14.8 %collective-permute-start.3 = (bf16[3,84,384]{2,1,0:T(8,128)(2,1)S(1)}, bf16[3,84,384]{2,1,0:T(8,128)(2,1)S(1)}, u32[]{:S(2)}, u32[]{:S(2)}) collective-permute-start(bf16[3,84,384]{2,1,0:T(8,128)(2,1)S(1)} %fusion.5), channel_id=1, source_target_pairs={{0,32},{32,64},{64,96},{96,128},{128,160},{160,192},{192,224},{224... | collective-permute-start | bytes 580616 | tf_op jit(solution)/shard_map/ppermute | solution.py:219

commit v2 on v1

v2 whole, which is shorter than its diff:
```python
import functools
import jax
import jax.numpy as jnp
from jax import lax
from jax.experimental import pallas as pl
from jax.experimental.pallas import tpu as pltpu
from jax.sharding import Mesh, PartitionSpec as P

HEADS = 6
WIN_LAT = 6
WIN_LON = 12
HEAD = 32
D = 192
PITCH = 16
TOK = WIN_LAT * PITCH
LANES = 128
SPAN = 256
norm_eps = 1e-05
clip_eps = 1e-06
masked = -1e30
AT_TABLE = 6 * D
AT_GAIN = AT_TABLE + 96
ROWS = 1280
LAT = ("y_lo", "z_hi", "z_lo")
LON = ("y_hi", "x", "core")
PARTS = (2, 4, 2, 4, 4, 2)
SLICED = ("y_lo", "z_lo", "x", "core")
WHOLE = (("z_hi", "y_hi"),)
highest = lax.Precision.HIGHEST
f32 = jnp.float32
bf16 = jnp.bfloat16

NT = (((1,), (1,)), ((), ()))
TN = (((0,), (0,)), ((), ()))


def nt(a, b, **kw):
    return lax.dot_general(a, b, NT, preferred_element_type=f32, **kw)


def tn(a, b, **kw):
    return lax.dot_general(a, b, TN, preferred_element_type=f32, **kw)


def nn(a, b, **kw):
    return jnp.dot(a, b, preferred_element_type=f32, **kw)


def iota(shape, dim):
    return lax.broadcasted_iota(jnp.int32, shape, dim)


def base_pattern():
    p = iota((SPAN, SPAN), 0)
    lane = iota((SPAN, SPAN), 1)
    d = lane // PITCH
    c = lane % PITCH
    hit = (p == (2 * WIN_LAT - 2 - d) * (2 * WIN_LON - 1) - c + WIN_LON - 1) & (c < WIN_LON) & (d < 2 * WIN_LAT - 1)
    return hit.astype(f32)


def kernel(windows, meta_ref, s_ref, g_ref, up_ref, side_ref, gain_ref, wqkv_ref, wproj_ref, table_ref,
           both_ref, grads_ref,
           xs, gs, tab, tilt, span, bias, un, nm, inv, q_s, k_s, v_s, dm_s, mix, dq_s, dk_s, dv_s, fold):
    half_lat = WIN_LAT // 2
    half_lon = WIN_LON // 2
    kinds = table_ref.shape[0] // HEADS

    tab[...] = jnp.zeros_like(tab)
    tab[:, :table_ref.shape[1]] = table_ref[...]
    for c in range(PITCH):
        moved = tab[...] if c == 0 else pltpu.roll(tab[...], SPAN - c, axis=1)
        for half in range(2):
            tilt[half, pl.ds(c, kinds * HEADS, stride=PITCH), :] = moved[:, half * LANES:(half + 1) * LANES]
    pattern = base_pattern()
    span[...] = nn(jnp.concatenate([tilt[0], tilt[1]], axis=1), pattern, precision=highest)
    slot = iota((PITCH, LANES), 1)
    open_slot = (slot % PITCH < WIN_LON) & (slot < TOK)
    split = meta_ref[windows] > 0

    def spread(n, carry):
        wide = span[pl.ds(pl.multiple_of(n * PITCH, PITCH), PITCH), :]
        for r in range(WIN_LAT):
            off = (WIN_LAT - 1 - r) * PITCH
            part = wide if off == 0 else pltpu.roll(wide, SPAN - off, axis=1)
            other = (slot < half_lat * PITCH) if r >= half_lat else (slot >= half_lat * PITCH)
            ok = open_slot & jnp.logical_not(split & other)
            bias[n % kinds, pl.ds(pl.multiple_of((n // kinds) * TOK + r * PITCH, PITCH), PITCH), :] = jnp.where(ok, part[:, :LANES], masked)
        return carry

    lax.fori_loop(0, kinds * HEADS, spread, 0)
    fold[...] = jnp.zeros_like(fold)

    xs[...] = jnp.zeros_like(xs)
    gs[...] = jnp.zeros_like(gs)
    for w in range(windows):
        for r in range(WIN_LAT):
            at = w * TOK + r * PITCH
            start = half_lon + w * WIN_LON
            inside = WIN_LON if w < windows - 1 else half_lon
            for dst, src, lo in ((xs, s_ref, 0), (gs, g_ref, D)):
                if r < half_lat:
                    dst[at:at + inside, :] = src[r + half_lat, start:start + inside, :]
                    if inside < WIN_LON:
                        dst[at + inside:at + WIN_LON, :] = side_ref[r, :, lo:lo + D]
                else:
                    dst[at:at + inside, :] = up_ref[r - half_lat, start:start + inside, lo:lo + D]
                    if inside < WIN_LON:
                        dst[at + inside:at + WIN_LON, :] = side_ref[r, :, lo:lo + D]

    gain = gain_ref[...]
    x = xs[...].astype(f32)
    centre = x - jnp.mean(x, axis=-1, keepdims=True)
    inverse = lax.rsqrt(jnp.mean(centre * centre, axis=-1, keepdims=True) + norm_eps)
    unit = centre * inverse
    un[...] = unit
    inv[...] = inverse
    normed = (unit * gain).astype(bf16)
    nm[...] = normed
    wq, wk, wv = (wqkv_ref[:, i * D:(i + 1) * D] for i in range(3))
    q_s[...] = nn(normed, wq).astype(bf16)
    k_s[...] = nn(normed, wk).astype(bf16)
    v_s[...] = nn(normed, wv).astype(bf16)
    dm_s[...] = nt(gs[...], wproj_ref[...]).astype(bf16)

    scale = HEAD ** (-0.5)
    head_of = iota((TOK, D), 1) // HEAD
    pads = jnp.zeros((LANES - TOK, D), bf16)

    def by_head(a):
        zero = jnp.zeros_like(a)
        return [jnp.where(head_of == h, a, zero) for h in range(HEADS)]

    def window(w, carry):
        rows = pl.ds(pl.multiple_of(w * TOK, TOK), TOK)
        kind = meta_ref[w]
        q, k, v, dm = q_s[rows, :], k_s[rows, :], v_s[rows, :], dm_s[rows, :]
        q_heads = jnp.concatenate(by_head(q), axis=0)
        dm_heads = jnp.concatenate(by_head(dm), axis=0)
        k_pad = jnp.concatenate([k, pads], axis=0)
        v_pad = jnp.concatenate([v, pads], axis=0)
        scores = nt(q_heads, k_pad) * scale + bias[kind]
        top = jnp.max(scores, axis=-1, keepdims=True)
        raised = jnp.exp(scores - top)
        probs = raised * (1.0 / jnp.sum(raised, axis=-1, keepdims=True))
        probs_low = probs.astype(bf16)
        d_probs = nt(dm_heads, v_pad)
        d_scores = probs * (d_probs - jnp.sum(probs * d_probs, axis=-1, keepdims=True))
        low = d_scores.astype(bf16)
        side = lambda a: jnp.concatenate([a[h * TOK:(h + 1) * TOK] for h in range(HEADS)], axis=1)
        tall = lambda a: jnp.concatenate([b for part in by_head(a) for b in (part, pads)], axis=0)
        mix[rows, :] = nn(side(probs_low), tall(v)).astype(bf16)
        dq_s[rows, :] = (nn(side(low), tall(k)) * scale).astype(bf16)
        dv_s[rows, :] = tn(probs_low, dm_heads)[:TOK].astype(bf16)
        dk_s[rows, :] = (tn(low, q_heads) * scale)[:TOK].astype(bf16)
        for h in range(HEADS):
            total = None
            for r in range(WIN_LAT):
                off = (WIN_LAT - 1 - r) * PITCH
                part = d_scores[h * TOK + r * PITCH:h * TOK + (r + 1) * PITCH]
                part = jnp.concatenate([part, jnp.zeros_like(part)], axis=1)
                if off:
                    part = pltpu.roll(part, off, axis=1)
                total = part if total is None else total + part
            fold[pl.ds(pl.multiple_of((h * kinds + kind) * PITCH, PITCH), PITCH), :] += total
        return carry

    lax.fori_loop(0, windows, window, 0)

    branch = nn(mix[...], wproj_ref[...]).astype(bf16)
    gp = tn(mix[...], gs[...]).astype(bf16)
    d_normed = nt(dq_s[...], wq) + nt(dk_s[...], wk) + nt(dv_s[...], wv)
    gq = []
    for i, d in enumerate((dq_s, dk_s, dv_s)):
        gq.append(tn(nm[...], d[...]).astype(bf16))
    gq = jnp.concatenate(gq, axis=1)
    for b in range(4):
        grads_ref[b * D:(b + 1) * D, :] = gq[:, b * LANES:(b + 1) * LANES]
    grads_ref[4 * D:5 * D, :] = jnp.concatenate([gq[:, 4 * LANES:], gp[:, LANES:]], axis=1)
    grads_ref[5 * D:6 * D, :] = gp[:, :LANES]
    unit = un[...]
    gg = jnp.sum(d_normed * unit, axis=0, keepdims=True)
    gg = jnp.concatenate([gg[:, :LANES], jnp.concatenate([gg[:, LANES:], jnp.zeros((1, SPAN - D), f32)], axis=1), jnp.zeros((ROWS - AT_GAIN - 2, LANES), f32)], axis=0)
    grads_ref[AT_GAIN:, :] = gg.astype(bf16)
    d_unit = d_normed * gain
    path = inv[...] * (d_unit - jnp.mean(d_unit, axis=-1, keepdims=True) - unit * jnp.mean(d_unit * unit, axis=-1, keepdims=True))
    path = path.astype(bf16)
    for w in range(windows):
        for r in range(WIN_LAT):
            at = w * TOK + r * PITCH
            both_ref[r, w * WIN_LON:(w + 1) * WIN_LON, 0:D] = branch[at:at + WIN_LON]
            both_ref[r, w * WIN_LON:(w + 1) * WIN_LON, D:2 * D] = path[at:at + WIN_LON]

    back = nt(fold[...], pattern, precision=highest)
    for half in range(2):
        tilt[half] = back[:, half * LANES:(half + 1) * LANES]
    total = None
    for c in range(WIN_LON):
        part = jnp.concatenate([tilt[half, pl.ds(c, kinds * HEADS, stride=PITCH), :] for half in range(2)], axis=1)
        if c:
            part = pltpu.roll(part, c, axis=1)
        total = part if total is None else total + part
    for half in range(2):
        at = AT_TABLE + half * kinds * HEADS
        grads_ref[at:at + kinds * HEADS, :] = total[:, half * LANES:(half + 1) * LANES].astype(bf16)


def attend(meta, s, g, up, side, gain, w_qkv, w_proj, table):
    windows = s.shape[1] // WIN_LON
    n = windows * TOK
    vm = pl.BlockSpec(memory_space=pltpu.VMEM)
    kh = table.shape[0]
    return pl.pallas_call(
        functools.partial(kernel, windows),
        out_shape=(
            jax.ShapeDtypeStruct(s.shape[:2] + (2 * D,), bf16),
            jax.ShapeDtypeStruct((ROWS, LANES), bf16),
        ),
        in_specs=[pl.BlockSpec(memory_space=pltpu.SMEM)] + [vm] * 8,
        out_specs=(vm,) * 2,
        scratch_shapes=[
            pltpu.VMEM((n, D), bf16), pltpu.VMEM((n, D), bf16), pltpu.VMEM((kh, SPAN), f32),
            pltpu.VMEM((2, kh * PITCH, LANES), f32), pltpu.VMEM((kh * PITCH, SPAN), f32),
            pltpu.VMEM((kh // HEADS, HEADS * TOK, LANES), f32),
            pltpu.VMEM((n, D), f32), pltpu.VMEM((n, D), bf16), pltpu.VMEM((n, 1), f32),
        ] + [pltpu.VMEM((n, D), bf16)] * 8 + [pltpu.VMEM((kh * PITCH, SPAN), f32)],
        cost_estimate=pl.CostEstimate(flops=2_000_000_000, bytes_accessed=4_000_000, transcendentals=500_000),
        name="attend",
    )(meta, s, g, up, side, gain, w_qkv, w_proj, table)


def finish_kernel(grads_ref, gq_ref, gp_ref, gt_ref, gg_ref):
    def scale_of(parts, count):
        total = sum(jnp.sum(jnp.sum(p * p, axis=0, keepdims=True), axis=1, keepdims=True) for p in parts)
        return jnp.minimum(1.0, lax.rsqrt(total / count + clip_eps))

    kh = gt_ref.shape[0]
    wide = [grads_ref[b * D:(b + 1) * D, :].astype(f32) for b in range(4)]
    shared = grads_ref[4 * D:5 * D, :].astype(f32)
    low, high = shared[:, :LANES // 2], shared[:, LANES // 2:]
    first = grads_ref[5 * D:6 * D, :].astype(f32)
    by = scale_of(wide + [low], gq_ref.shape[0] * gq_ref.shape[1])
    for b in range(4):
        gq_ref[:, b * LANES:(b + 1) * LANES] = wide[b] * by
    gq_ref[:, 4 * LANES:] = low * by
    by = scale_of([first, high], gp_ref.shape[0] * gp_ref.shape[1])
    gp_ref[:, :LANES] = first * by
    gp_ref[:, LANES:] = high * by
    left = grads_ref[AT_TABLE:AT_TABLE + kh, :].astype(f32)
    right = grads_ref[AT_TABLE + kh:AT_TABLE + 2 * kh, :].astype(f32)
    by = scale_of([left, right], kh * gt_ref.shape[1])
    gt_ref[:, :LANES] = left * by
    gt_ref[:, LANES:] = (right * by)[:, :gt_ref.shape[1] - LANES]
    rows = grads_ref[AT_GAIN:AT_GAIN + 16, :].astype(f32)
    by = scale_of([rows], D)
    gg_ref[:, :LANES] = rows[0:1] * by
    gg_ref[:, LANES:] = (rows[1:2] * by)[:, :D - LANES]


def finish(grads, table_rows, extent):
    vm = pl.BlockSpec(memory_space=pltpu.VMEM)
    return pl.pallas_call(
        finish_kernel,
        out_shape=(
            jax.ShapeDtypeStruct((D, 3 * D), f32),
            jax.ShapeDtypeStruct((D, D), f32),
            jax.ShapeDtypeStruct((table_rows, extent), f32),
            jax.ShapeDtypeStruct((1, D), f32),
        ),
        in_specs=[vm],
        out_specs=(vm,) * 4,
        cost_estimate=pl.CostEstimate(flops=1_000_000, bytes_accessed=1_000_000, transcendentals=4),
        name="finish",
    )(grads)


def shifted(value, axis, steps):
    count = lax.axis_size(axis)
    return lax.ppermute(value, axis, [(i, (i + steps) % count) for i in range(count)])


def spread_sum(part, axes):
    n = lax.axis_size(axes)
    got = lax.all_to_all(part.reshape(n, -1, LANES), axes, 0, 0, tiled=True)
    return jnp.sum(got.astype(f32), axis=0).astype(bf16)


def collect(part, axes):
    n = lax.axis_size(axes)
    return lax.all_to_all(jnp.broadcast_to(part[None], (n,) + part.shape), axes, 0, 0, tiled=True)


def total_of(packed):
    part = spread_sum(packed, SLICED)
    for axes in WHOLE:
        part = jnp.sum(collect(part, axes).astype(f32), axis=0).astype(bf16)
    return collect(part, SLICED).reshape(-1, LANES)


def on_device(state_grid, norm_gain, w_qkv, w_proj, bias_table, window_kind, cotangent):
    rows_dev, cols_dev, channels = state_grid.shape
    half_lat, half_lon = WIN_LAT // 2, WIN_LON // 2
    lat, lon = lax.axis_index(LAT), lax.axis_index(LON)
    windows = cols_dev // WIN_LON
    joint = jnp.concatenate([state_grid[:half_lat], cotangent[:half_lat]], axis=2)
    up = shifted(joint, LAT, -1)
    side = jnp.concatenate([state_grid[half_lat:, :half_lon], cotangent[half_lat:, :half_lon]], axis=2)
    side = shifted(jnp.concatenate([side, up[:, :half_lon]], axis=0), LON, -1)
    kinds = lax.dynamic_slice(window_kind, (lat, lon * windows), (1, windows))[0]
    last = (lat == lax.axis_size(LAT) - 1).astype(jnp.int32)
    meta = jnp.concatenate([kinds, last[None]])
    kind_count, heads, extent = bias_table.shape
    table = bias_table.transpose(1, 0, 2).reshape(heads * kind_count, extent)
    both, packed = attend(meta, state_grid, cotangent, up, side, norm_gain.reshape(1, -1), w_qkv, w_proj, table)
    moved = shifted(both[:, -half_lon:], LON, 1)
    placed = jnp.concatenate([moved, both[:, :-half_lon]], axis=1)
    lower = shifted(placed[half_lat:], LAT, 1)
    own = jnp.concatenate([lower, placed[:half_lat]], axis=0).astype(f32)
    out_field = (state_grid.astype(f32) + own[:, :, :channels]).astype(bf16)
    d_field = (cotangent.astype(f32) + own[:, :, channels:]).astype(bf16)
    gq, gp, gt, gg = finish(total_of(packed), heads * kind_count, extent)
    gt = gt.reshape(heads, kind_count, extent).transpose(1, 0, 2)
    return (out_field, d_field, gq, gp, gt, gg.reshape(-1))


def solution(mesh):
    in_specs = (P(LAT, LON, None), P(), P(), P(), P(), P(), P(LAT, LON, None))
    out_specs = (P(LAT, LON, None), P(LAT, LON, None), P(), P(), P(), P())
    mesh = Mesh(mesh.devices.reshape(PARTS), LAT + LON)
    return jax.shard_map(on_device, mesh=mesh, in_specs=in_specs, out_specs=out_specs, check_vma=False)
```

time: 130 us -> 103 us (0.79)
  blocking collectives: 34.4 us -> 15.7 us
  local copies, waits for them, and re-layouts: 10.9 us -> 4.04 us
  other arithmetic: 8.14 us -> 2.05 us
  starting transfers between devices: 32.5 us -> 38.2 us
  between operations: 3.74 us -> 0.86 us
  Pallas kernels: 16.9 us -> 18.9 us
    all_to_all x2 -> x1, blocking collectives: 34.4 us -> 15.7 us  [spread_sum(): got = lax.all_to_all(part.reshape(n, -1, LANES), axes, 0, 0, tiled=True)]
    all_to_all x2, starting transfers between devices: 9.61 us -> 16.2 us  [collect(): lax.all_to_all(jnp.broadcast_to(part[None], (n,) + part.shape), axes, 0,...]
    reduce_sum x6 -> x2, other arithmetic: 2.75 us -> 0.09 us  [the longest x1 0.06 us: spread_sum(): return jnp.sum(got.astype(f32), axis=0).astype(bf16)]
    all_to_all x2, waiting for transfers between devices: 6.19 us -> 8.74 us  [collect(): lax.all_to_all(jnp.broadcast_to(part[None], (n,) + part.shape), axes, 0,...]
    ppermute x4, waiting for transfers between devices: 16.4 us -> 14 us  [shifted(): lax.ppermute(value, axis, [(i, (i + steps) % count) for i in range(count)])]
    pallas_call x0 -> x1, Pallas kernels: none -> 2.05 us  [finish(): pl.pallas_call(finish_kernel, out_shape=(jax.ShapeDtypeStruct((D, 3 * D),...]
    mul x3 -> x0, local copies, waits for them, and re-layouts: 1.88 us -> none  [clip_rms(): gradient * jnp.minimum(1.0, lax.rsqrt(jnp.sum(gradient * gradient) / coun...]
    concatenate x1 -> x0, local copies, waits for them, and re-layouts: 1.7 us -> none  [on_device(): flat = jnp.concatenate([p.astype(bf16).ravel() for p in pieces])]
where the time goes in v2:
time: 103 us; the launch traced here: 102 us
  starting transfers between devices  38.2 us (37%)
  waiting for transfers between devices  22.7 us (22%)
  Pallas kernels  18.9 us (18%)
  blocking collectives  15.7 us (15%)
  local copies, waits for them, and re-layouts  4.04 us (4%)
  other arithmetic  2.05 us (2%)
    ppermute x4, starting transfers between devices, shifted(): lax.ppermute(value, axis, [(i, (i + steps) % count) for i in range(count)])  22 us
    pallas_call x1, Pallas kernels, attend(): pl.pallas_call(functools.partial(kernel, windows), out_shape=(jax.ShapeDt...  16.8 us
    all_to_all x2, starting transfers between devices, collect(): lax.all_to_all(jnp.broadcast_to(part[None], (n,) + part.shape), axes, 0,...  16.2 us
    all_to_all x1, blocking collectives, spread_sum(): got = lax.all_to_all(part.reshape(n, -1, LANES), axes, 0, 0, tiled=True)  15.7 us
    ppermute x4, waiting for transfers between devices, shifted(): lax.ppermute(value, axis, [(i, (i + steps) % count) for i in range(count)])  14 us
    all_to_all x2, waiting for transfers between devices, collect(): lax.all_to_all(jnp.broadcast_to(part[None], (n,) + part.shape), axes, 0,...  8.74 us
  transfers between devices with their start and end apart: 6, of which 4 were waited for; matrix products, arithmetic and copies ran while one was open for 3% of the time, Pallas kernels for 0%

profile of v2, /device:TPU:1, one launch (start us, length us, event | category | flops | bytes accessed | tf_op | source)
XLA Modules:
  0.0 102.4 jit_solution(8387400451304869422)
XLA Ops:
  0.6 0.0 copy-start
  0.6 0.0 copy-start.4
  0.7 0.0 slice-start
  0.7 1.0 slice-done
  1.7 0.1 slice-done.1
  1.7 0.1 pad_maximum_fusion.1
  1.8 12.5 %collective-permute-start = (bf16[3,84,384]{2,1,0:T(8,128)(2,1)S(1)}, bf16[3,84,384]{2,1,0:T(8,128)(2,1)S(1)}, u32[]{:S(2)}, u32[]{:S(2)}) collective-permute-start(bf16[3,84,384]{2,1,0:T(8,128)(2,1)S(1)} %pad_maximum_fusion.1), channel_id=1, source_target_pairs={{0,480},{32,0},{64,32},{96,64},{128,96},{160,128},{192,160},{224,1... | collective-permute-start | bytes 580616 | tf_op jit(solution)/shard_map/ppermute | solution.py:279
  14.4 0.1 dynamic-slice_bitcast_fusion
  14.5 3.5 %collective-permute-done.up_ref = bf16[3,84,384]{2,1,0:T(8,128)(2,1)S(1)} collective-permute-done((bf16[3,84,384]{2,1,0:T(8,128)(2,1)S(1)}, bf16[3,84,384]{2,1,0:T(8,128)(2,1)S(1)}, u32[]{:S(2)}, u32[]{:S(2)}) %collective-permute-start) | collective-permute-done | bytes 193568 | tf_op jit(solution)/shard_map/ppermute | solution.py:279
  18.1 0.1 pad_maximum_fusion.2
  18.1 3.4 %collective-permute-start.1 = (bf16[6,6,384]{2,1,0:T(8,128)(2,1)S(1)}, bf16[6,6,384]{2,1,0:T(8,128)(2,1)S(1)}, u32[]{:S(2)}, u32[]{:S(2)}) collective-permute-start(bf16[6,6,384]{2,1,0:T(8,128)(2,1)S(1)} %pad_maximum_fusion.2), channel_id=1, source_target_pairs={{0,31},{1,0},{2,1},{3,2},{4,3},{5,4},{6,5},{7,6},{8,7},{9,8},{10,9... | collective-permute-start | bytes 82952 | tf_op jit(solution)/shard_map/ppermute | solution.py:279
  21.6 0.6 pad_add_fusion.meta_ref
  22.2 2.1 %collective-permute-done.1.side_ref = bf16[6,6,384]{2,1,0:T(8,128)(2,1)S(1)} collective-permute-done((bf16[6,6,384]{2,1,0:T(8,128)(2,1)S(1)}, bf16[6,6,384]{2,1,0:T(8,128)(2,1)S(1)}, u32[]{:S(2)}, u32[]{:S(2)}) %collective-permute-start.1) | collective-permute-done | bytes 27680 | tf_op jit(solution)/shard_map/ppermute | solution.py:279
  24.3 0.6 copy-done.8
  24.9 16.8 %attend.1 = (bf16[6,84,384]{2,1,0:T(8,128)(2,1)}, bf16[1280,128]{1,0:T(8,128)(2,1)}) custom-call(s32[8]{0:T(128)} %pad_add_fusion.meta_ref, bf16[6,84,192]{2,1,0:T(8,128)(2,1)} %s_ref.1, bf16[6,84,192]{2,1,0:T(8,128)(2,1)} %g_ref.1, bf16[3,84,384]{2,1,0:T(8,128)(2,1)} %copy-done.7, bf16[6,6,384]{2,1,0:T(8,128)(2,1)} %copy-done.8, f32[1,192]{1,0:T(1,128)} %bitcast.17, ...), custom_call_target="tpu_custom_call" | custom-call | flops 2000000000 | bytes 4000000 | tf_op jit(solution)/shard_map/attend/pallas_call | solution.py:213
  41.7 15.7 %all_to_all.15 = bf16[32,40,128]{2,1,0:T(8,128)(2,1)S(1)} all-to-all(bf16[32,40,128]{2,1,0:T(8,128)(2,1)} %bitcast.14), channel_id=1, replica_groups=mesh['y_lo'=2,'z_hi'=4,'z_lo'=2,'y_hi'=4,'x'=4,'core'=2] {'y_lo','z_lo',..., dimensions={0} | all-to-all | bytes 655360 | tf_op jit(solution)/shard_map/all_to_all | solution.py:284
  57.4 0.1 reduce_sum.24
  57.5 0.7 broadcast_in_dim.20
  58.2 10.9 %all-to-all-start.1 = ((bf16[16,40,128]{2,1,0:T(8,128)(2,1)}), bf16[16,40,128]{2,1,0:T(8,128)(2,1)S(1)}, u32[]{:S(2)}, u32[]{:S(2)}) async-start(bf16[16,40,128]{2,1,0:T(8,128)(2,1)} %broadcast_in_dim.20), calls=%async_computation.1 | async-start | bytes 327680 | tf_op jit(solution)/shard_map/all_to_all | solution.py:290
  69.1 2.6 %collective-permute-start.2 = (bf16[6,6,384]{2,1,0:T(8,128)(2,1)S(1)}, bf16[6,6,384]{2,1,0:T(8,128)(2,1)S(1)}, u32[]{:S(2)}, u32[]{:S(2)}) collective-permute-start(bf16[6,6,384]{2,1,0:T(8,128)(2,1)S(1)} %slice.38), channel_id=1, source_target_pairs={{0,1},{1,2},{2,3},{3,4},{4,5},{5,6},{6,7},{7,8},{8,9},{9,10},{10,1... | collective-permute-start | bytes 82952 | tf_op jit(solution)/shard_map/ppermute | solution.py:279
  71.8 8.7 %all-to-all-done.1 = bf16[16,40,128]{2,1,0:T(8,128)(2,1)S(1)} async-done(((bf16[16,40,128]{2,1,0:T(8,128)(2,1)}), bf16[16,40,128]{2,1,0:T(8,128)(2,1)S(1)}, u32[]{:S(2)}, u32[]{:S(2)}) %all-to-all-start.1) | async-done | bytes 163872 | tf_op jit(solution)/shard_map/all_to_all | solution.py:290
  80.6 0.8 broadcast_in_dim.21
  81.3 5.3 %all-to-all-start.2 = ((bf16[32,40,128]{2,1,0:T(8,128)(2,1)}), bf16[32,40,128]{2,1,0:T(8,128)(2,1)S(1)}, u32[]{:S(2)}, u32[]{:S(2)}) async-start(bf16[32,40,128]{2,1,0:T(8,128)(2,1)} %broadcast_in_dim.21), calls=%async_computation.2 | async-start | bytes 655360 | tf_op jit(solution)/shard_map/all_to_all | solution.py:290
  86.6 0.1 fusion.4
  86.7 0.0 copy-start.3
  86.7 0.0 copy-start.5
  86.7 3.4 %collective-permute-start.3 = (bf16[3,84,384]{2,1,0:T(8,128)(2,1)S(1)}, bf16[3,84,384]{2,1,0:T(8,128)(2,1)S(1)}, u32[]{:S(2)}, u32[]{:S(2)}) collective-permute-start(bf16[3,84,384]{2,1,0:T(8,128)(2,1)S(1)} %fusion.4), channel_id=1, source_target_pairs={{0,32},{32,64},{64,96},{96,128},{128,160},{160,192},{192,224},{224... | collective-permute-start | bytes 580616 | tf_op jit(solution)/shard_map/ppermute | solution.py:279
  90.2 8.3 %collective-permute-done.3 = bf16[3,84,384]{2,1,0:T(8,128)(2,1)S(1)} collective-permute-done((bf16[3,84,384]{2,1,0:T(8,128)(2,1)S(1)}, bf16[3,84,384]{2,1,0:T(8,128)(2,1)S(1)}, u32[]{:S(2)}, u32[]{:S(2)}) %collective-permute-start.3) | collective-permute-done | bytes 193568 | tf_op jit(solution)/shard_map/ppermute | solution.py:279
  98.5 0.1 fusion.3
  98.6 1.1 %fusion = (bf16[6,84,192]{2,1,0:T(8,128)(2,1)}, bf16[6,84,192]{2,1,0:T(8,128)(2,1)}) fusion(f32[6,84,384]{2,1,0:T(8,128)S(1)} %fusion.3, bf16[6,84,192]{2,1,0:T(8,128)(2,1)S(1)} %copy-done.5, bf16[6,84,192]{2,1,0:T(8,128)(2,1)S(1)} %copy-done.3), kind=kLoop, calls=%fused_computation.1 | loop fusion | flops 580608 | bytes 1548288 | tf_op jit(solution)/shard_map/convert_element_type | solution.py:320
  99.6 0.7 copy-done.1
  100.3 2.0 %finish.1 = (f32[192,576]{1,0:T(8,128)}, f32[192,192]{1,0:T(8,128)}, f32[48,253]{1,0:T(8,128)}, f32[1,192]{1,0:T(1,128)}) custom-call(bf16[1280,128]{1,0:T(8,128)(2,1)} %bitcast.13), custom_call_target="tpu_custom_call" | custom-call | flops 1000000 | bytes 1000000 | tf_op jit(solution)/shard_map/finish/pallas_call | solution.py:262
  (21 shorter events, 0.1 us)
Async XLA Ops:
  0.6 13.8 %copy-start = (s32[16,224]{1,0:T(8,128)S(1)}, s32[16,224]{1,0:T(8,128)}, u32[]{:S(2)}) copy-start(s32[16,224]{1,0:T(8,128)} %param.12) | copy-start | bytes 43012
  0.6 13.7 %copy-start.4 = (bf16[6,84,192]{2,1,0:T(8,128)(2,1)S(1)}, bf16[6,84,192]{2,1,0:T(8,128)(2,1)}, u32[]{:S(2)}) copy-start(bf16[6,84,192]{2,1,0:T(8,128)(2,1)} %g_ref.1) | copy-start | bytes 580612
  0.7 1.0 slice-start
  0.7 1.1 %slice-start.1 = ((bf16[6,84,192]{2,1,0:T(8,128)(2,1)}), bf16[3,84,192]{2,1,0:T(8,128)(2,1)S(1)}, s32[]{:S(2)}) async-start(bf16[6,84,192]{2,1,0:T(8,128)(2,1)} %g_ref.1), calls=%async_computation.4 | async-start | bytes 270336 | tf_op jit(solution)/shard_map/slice | solution.py:305
  1.7 12.6 %copy-start.2 = (bf16[6,84,192]{2,1,0:T(8,128)(2,1)S(1)}, bf16[6,84,192]{2,1,0:T(8,128)(2,1)}, u32[]{:S(2)}) copy-start(bf16[6,84,192]{2,1,0:T(8,128)(2,1)} %s_ref.1) | copy-start | bytes 580612
  1.8 16.2 %collective-permute-start = (bf16[3,84,384]{2,1,0:T(8,128)(2,1)S(1)}, bf16[3,84,384]{2,1,0:T(8,128)(2,1)S(1)}, u32[]{:S(2)}, u32[]{:S(2)}) collective-permute-start(bf16[3,84,384]{2,1,0:T(8,128)(2,1)S(1)} %pad_maximum_fusion.1), channel_id=1, source_target_pairs={{0,480},{32,0},{64,32},{96,64},{128,96},{160,128},{192,160},{224,1... | collective-permute-start | bytes 580616 | tf_op jit(solution)/shard_map/ppermute | solution.py:279
  18.0 6.2 %copy-start.7 = (bf16[3,84,384]{2,1,0:T(8,128)(2,1)}, bf16[3,84,384]{2,1,0:T(8,128)(2,1)S(1)}, u32[]{:S(2)}) copy-start(bf16[3,84,384]{2,1,0:T(8,128)(2,1)S(1)} %collective-permute-done.up_ref) | copy-start | bytes 580612
  18.1 6.2 %collective-permute-start.1 = (bf16[6,6,384]{2,1,0:T(8,128)(2,1)S(1)}, bf16[6,6,384]{2,1,0:T(8,128)(2,1)S(1)}, u32[]{:S(2)}, u32[]{:S(2)}) collective-permute-start(bf16[6,6,384]{2,1,0:T(8,128)(2,1)S(1)} %pad_maximum_fusion.2), channel_id=1, source_target_pairs={{0,31},{1,0},{2,1},{3,2},{4,3},{5,4},{6,5},{7,6},{8,7},{9,8},{10,9... | collective-permute-start | bytes 82952 | tf_op jit(solution)/shard_map/ppermute | solution.py:279
  24.3 0.6 copy-start.8
  57.4 11.7 %copy-start.6 = (bf16[6,84,384]{2,1,0:T(8,128)(2,1)S(1)}, bf16[6,84,384]{2,1,0:T(8,128)(2,1)}, u32[]{:S(2)}) copy-start(bf16[6,84,384]{2,1,0:T(8,128)(2,1)} %get-tuple-element.12) | copy-start | bytes 1161220
  58.2 22.4 %all-to-all-start.1 = ((bf16[16,40,128]{2,1,0:T(8,128)(2,1)}), bf16[16,40,128]{2,1,0:T(8,128)(2,1)S(1)}, u32[]{:S(2)}, u32[]{:S(2)}) async-start(bf16[16,40,128]{2,1,0:T(8,128)(2,1)} %broadcast_in_dim.20), calls=%async_computation.1 | async-start | bytes 327680 | tf_op jit(solution)/shard_map/all_to_all | solution.py:290
  69.1 17.5 %collective-permute-start.2 = (bf16[6,6,384]{2,1,0:T(8,128)(2,1)S(1)}, bf16[6,6,384]{2,1,0:T(8,128)(2,1)S(1)}, u32[]{:S(2)}, u32[]{:S(2)}) collective-permute-start(bf16[6,6,384]{2,1,0:T(8,128)(2,1)S(1)} %slice.38), channel_id=1, source_target_pairs={{0,1},{1,2},{2,3},{3,4},{4,5},{5,6},{6,7},{7,8},{8,9},{9,10},{10,1... | collective-permute-start | bytes 82952 | tf_op jit(solution)/shard_map/ppermute | solution.py:279
  81.3 18.3 %all-to-all-start.2 = ((bf16[32,40,128]{2,1,0:T(8,128)(2,1)}), bf16[32,40,128]{2,1,0:T(8,128)(2,1)S(1)}, u32[]{:S(2)}, u32[]{:S(2)}) async-start(bf16[32,40,128]{2,1,0:T(8,128)(2,1)} %broadcast_in_dim.21), calls=%async_computation.2 | async-start | bytes 655360 | tf_op jit(solution)/shard_map/all_to_all | solution.py:290
  86.7 11.9 %copy-start.3 = (bf16[6,84,192]{2,1,0:T(8,128)(2,1)S(1)}, bf16[6,84,192]{2,1,0:T(8,128)(2,1)}, u32[]{:S(2)}) copy-start(bf16[6,84,192]{2,1,0:T(8,128)(2,1)} %s_ref.1) | copy-start | bytes 580612
  86.7 11.9 %copy-start.5 = (bf16[6,84,192]{2,1,0:T(8,128)(2,1)S(1)}, bf16[6,84,192]{2,1,0:T(8,128)(2,1)}, u32[]{:S(2)}) copy-start(bf16[6,84,192]{2,1,0:T(8,128)(2,1)} %g_ref.1) | copy-start | bytes 580612
  86.7 11.8 %collective-permute-start.3 = (bf16[3,84,384]{2,1,0:T(8,128)(2,1)S(1)}, bf16[3,84,384]{2,1,0:T(8,128)(2,1)S(1)}, u32[]{:S(2)}, u32[]{:S(2)}) collective-permute-start(bf16[3,84,384]{2,1,0:T(8,128)(2,1)S(1)} %fusion.4), channel_id=1, source_target_pairs={{0,32},{32,64},{64,96},{96,128},{128,160},{160,192},{192,224},{224... | collective-permute-start | bytes 580616 | tf_op jit(solution)/shard_map/ppermute | solution.py:279
  99.6 0.7 copy-start.1

commit v3 on v2

--- a/solution.py
+++ b/solution.py
@@ -21,6 +21,8 @@
 AT_TABLE = 6 * D
 AT_GAIN = AT_TABLE + 96
 ROWS = 1280
+VM_ATTEND = 28
+VM_FINISH = 8
 LAT = ("y_lo", "z_hi", "z_lo")
 LON = ("y_hi", "x", "core")
 PARTS = (2, 4, 2, 4, 4, 2)
@@ -88,7 +90,7 @@
             bias[n % kinds, pl.ds(pl.multiple_of((n // kinds) * TOK + r * PITCH, PITCH), PITCH), :] = jnp.where(ok, part[:, :LANES], masked)
         return carry
 
-    lax.fori_loop(0, kinds * HEADS, spread, 0)
+    lax.fori_loop(0, kinds * HEADS, spread, 0, unroll=True)
     fold[...] = jnp.zeros_like(fold)
 
     xs[...] = jnp.zeros_like(xs)
@@ -131,8 +133,8 @@
         zero = jnp.zeros_like(a)
         return [jnp.where(head_of == h, a, zero) for h in range(HEADS)]
 
-    def window(w, carry):
-        rows = pl.ds(pl.multiple_of(w * TOK, TOK), TOK)
+    def window(w):
+        rows = pl.ds(w * TOK, TOK)
         kind = meta_ref[w]
         q, k, v, dm = q_s[rows, :], k_s[rows, :], v_s[rows, :], dm_s[rows, :]
         q_heads = jnp.concatenate(by_head(q), axis=0)
@@ -163,9 +165,9 @@
                     part = pltpu.roll(part, off, axis=1)
                 total = part if total is None else total + part
             fold[pl.ds(pl.multiple_of((h * kinds + kind) * PITCH, PITCH), PITCH), :] += total
-        return carry
-
-    lax.fori_loop(0, windows, window, 0)
+
+    for w in range(windows):
+        window(w)
 
     branch = nn(mix[...], wproj_ref[...]).astype(bf16)
     gp = tn(mix[...], gs[...]).astype(bf16)
@@ -225,6 +227,7 @@
             pltpu.VMEM((n, D), f32), pltpu.VMEM((n, D), bf16), pltpu.VMEM((n, 1), f32),
         ] + [pltpu.VMEM((n, D), bf16)] * 8 + [pltpu.VMEM((kh * PITCH, SPAN), f32)],
         cost_estimate=pl.CostEstimate(flops=2_000_000_000, bytes_accessed=4_000_000, transcendentals=500_000),
+        compiler_params=pltpu.CompilerParams(vmem_limit_bytes=VM_ATTEND << 20),
         name="attend",
     )(meta, s, g, up, side, gain, w_qkv, w_proj, table)
 
@@ -270,6 +273,7 @@
         in_specs=[vm],
         out_specs=(vm,) * 4,
         cost_estimate=pl.CostEstimate(flops=1_000_000, bytes_accessed=1_000_000, transcendentals=4),
+        compiler_params=pltpu.CompilerParams(vmem_limit_bytes=VM_FINISH << 20),
         name="finish",
     )(grads)
 
@@ -290,11 +294,13 @@
     return lax.all_to_all(jnp.broadcast_to(part[None], (n,) + part.shape), axes, 0, 0, tiled=True)
 
 
-def total_of(packed):
+def total_of(packed, ahead, further):
     part = spread_sum(packed, SLICED)
+    part, ahead = lax.optimization_barrier((part, ahead))
     for axes in WHOLE:
         part = jnp.sum(collect(part, axes).astype(f32), axis=0).astype(bf16)
-    return collect(part, SLICED).reshape(-1, LANES)
+    part, ahead = lax.optimization_barrier((part, further(ahead)))
+    return collect(part, SLICED).reshape(-1, LANES), ahead
 
 
 def on_device(state_grid, norm_gain, w_qkv, w_proj, bias_table, window_kind, cotangent):
@@ -313,12 +319,16 @@
     table = bias_table.transpose(1, 0, 2).reshape(heads * kind_count, extent)
     both, packed = attend(meta, state_grid, cotangent, up, side, norm_gain.reshape(1, -1), w_qkv, w_proj, table)
     moved = shifted(both[:, -half_lon:], LON, 1)
-    placed = jnp.concatenate([moved, both[:, :-half_lon]], axis=1)
-    lower = shifted(placed[half_lat:], LAT, 1)
-    own = jnp.concatenate([lower, placed[:half_lat]], axis=0).astype(f32)
+
+    def up_to_rows(moved):
+        placed = jnp.concatenate([moved, both[:, :-half_lon]], axis=1)
+        return placed[:half_lat], shifted(placed[half_lat:], LAT, 1)
+
+    summed, (stay, lower) = total_of(packed, moved, up_to_rows)
+    own = jnp.concatenate([lower, stay], axis=0).astype(f32)
     out_field = (state_grid.astype(f32) + own[:, :, :channels]).astype(bf16)
     d_field = (cotangent.astype(f32) + own[:, :, channels:]).astype(bf16)
-    gq, gp, gt, gg = finish(total_of(packed), heads * kind_count, extent)
+    gq, gp, gt, gg = finish(summed, heads * kind_count, extent)
     gt = gt.reshape(heads, kind_count, extent).transpose(1, 0, 2)
     return (out_field, d_field, gq, gp, gt, gg.reshape(-1))
 

time: 103 us -> 92.7 us (0.900)
  blocking collectives: 15.7 us -> 0 us
  Pallas kernels: 18.9 us -> 11.3 us
  starting transfers between devices: 38.2 us -> 45.8 us
  waiting for transfers between devices: 22.7 us -> 29.4 us
    all_to_all x1 -> x0, blocking collectives: 15.7 us -> none  [spread_sum(): got = lax.all_to_all(part.reshape(n, -1, LANES), axes, 0, 0, tiled=True)]
    all_to_all x2, waiting for transfers between devices: 8.74 us -> 17.5 us  [collect(): lax.all_to_all(jnp.broadcast_to(part[None], (n,) + part.shape), axes, 0,...]
    ppermute x4, waiting for transfers between devices: 14 us -> 6.58 us  [shifted(): lax.ppermute(value, axis, [(i, (i + steps) % count) for i in range(count)])]
    all_to_all x0 -> x1, starting transfers between devices: none -> 6.7 us  [spread_sum(): got = lax.all_to_all(part.reshape(n, -1, LANES), axes, 0, 0, tiled=True)]
    pallas_call x1, Pallas kernels: 16.8 us -> 10.2 us  [attend(): pl.pallas_call(functools.partial(kernel, windows), out_shape=(jax.ShapeDt...]
    all_to_all x0 -> x1, waiting for transfers between devices: none -> 5.34 us  [spread_sum(): got = lax.all_to_all(part.reshape(n, -1, LANES), axes, 0, 0, tiled=True)]
  transfers between devices with their start and end apart: 6 -> 7, of which waited for: 4 -> 6; matrix products, arithmetic and copies ran while one was open for 3% -> 2% of each run, Pallas kernels for 0% -> 0%
where the time goes in v3:
time: 92.7 us; the launch traced here: 92.2 us
  starting transfers between devices  45.8 us (49%)
  waiting for transfers between devices  29.4 us (32%)
  Pallas kernels  11.3 us (12%)
  local copies, waits for them, and re-layouts  3.36 us (4%)
  other arithmetic  1.59 us (2%)
    ppermute x4, starting transfers between devices, shifted(): lax.ppermute(value, axis, [(i, (i + steps) % count) for i in range(count)])  21.9 us
    all_to_all x2, waiting for transfers between devices, collect(): lax.all_to_all(jnp.broadcast_to(part[None], (n,) + part.shape), axes, 0,...  17.5 us
    all_to_all x2, starting transfers between devices, collect(): lax.all_to_all(jnp.broadcast_to(part[None], (n,) + part.shape), axes, 0,...  17.2 us
    pallas_call x1, Pallas kernels, attend(): pl.pallas_call(functools.partial(kernel, windows), out_shape=(jax.ShapeDt...  10.2 us
    all_to_all x1, starting transfers between devices, spread_sum(): got = lax.all_to_all(part.reshape(n, -1, LANES), axes, 0, 0, tiled=True)  6.7 us
    ppermute x4, waiting for transfers between devices, shifted(): lax.ppermute(value, axis, [(i, (i + steps) % count) for i in range(count)])  6.58 us
    all_to_all x1, waiting for transfers between devices, spread_sum(): got = lax.all_to_all(part.reshape(n, -1, LANES), axes, 0, 0, tiled=True)  5.34 us
  transfers between devices with their start and end apart: 7, of which 6 were waited for; matrix products, arithmetic and copies ran while one was open for 2% of the time, Pallas kernels for 0%

profile of v3, /device:TPU:1, one launch (start us, length us, event | category | flops | bytes accessed | tf_op | source)
XLA Modules:
  0.0 92.2 jit_solution(14887301264329390984)
XLA Ops:
  0.6 0.0 copy-start
  0.7 0.0 slice-start
  0.7 0.0 slice-start.1
  0.7 1.0 %slice-done = bf16[3,84,192]{2,1,0:T(8,128)(2,1)S(1)} async-done(((bf16[6,84,192]{2,1,0:T(8,128)(2,1)}), bf16[3,84,192]{2,1,0:T(8,128)(2,1)S(1)}, s32[]{:S(2)}) %slice-start) | async-done | bytes 96792 | tf_op jit(solution)/shard_map/slice | solution.py:311
  1.7 0.1 slice-done.1
  1.7 0.1 pad_maximum_fusion.1
  1.8 12.6 %collective-permute-start = (bf16[3,84,384]{2,1,0:T(8,128)(2,1)S(1)}, bf16[3,84,384]{2,1,0:T(8,128)(2,1)S(1)}, u32[]{:S(2)}, u32[]{:S(2)}) collective-permute-start(bf16[3,84,384]{2,1,0:T(8,128)(2,1)S(1)} %pad_maximum_fusion.1), channel_id=1, source_target_pairs={{0,480},{32,0},{64,32},{96,64},{128,96},{160,128},{192,160},{224,1... | collective-permute-start | bytes 580616 | tf_op jit(solution)/shard_map/ppermute | solution.py:283
  14.5 0.0 copy-start.4
  14.6 0.1 dynamic-slice_bitcast_fusion
  14.7 3.5 %collective-permute-done.up_ref = bf16[3,84,384]{2,1,0:T(8,128)(2,1)S(1)} collective-permute-done((bf16[3,84,384]{2,1,0:T(8,128)(2,1)S(1)}, bf16[3,84,384]{2,1,0:T(8,128)(2,1)S(1)}, u32[]{:S(2)}, u32[]{:S(2)}) %collective-permute-start) | collective-permute-done | bytes 193568 | tf_op jit(solution)/shard_map/ppermute | solution.py:283
  18.2 0.1 pad_maximum_fusion.2
  18.3 3.4 %collective-permute-start.1 = (bf16[6,6,384]{2,1,0:T(8,128)(2,1)S(1)}, bf16[6,6,384]{2,1,0:T(8,128)(2,1)S(1)}, u32[]{:S(2)}, u32[]{:S(2)}) collective-permute-start(bf16[6,6,384]{2,1,0:T(8,128)(2,1)S(1)} %pad_maximum_fusion.2), channel_id=1, source_target_pairs={{0,31},{1,0},{2,1},{3,2},{4,3},{5,4},{6,5},{7,6},{8,7},{9,8},{10,9... | collective-permute-start | bytes 82952 | tf_op jit(solution)/shard_map/ppermute | solution.py:283
  21.7 0.1 pad_add_fusion.meta_ref
  21.8 2.6 %collective-permute-done.1.side_ref = bf16[6,6,384]{2,1,0:T(8,128)(2,1)S(1)} collective-permute-done((bf16[6,6,384]{2,1,0:T(8,128)(2,1)S(1)}, bf16[6,6,384]{2,1,0:T(8,128)(2,1)S(1)}, u32[]{:S(2)}, u32[]{:S(2)}) %collective-permute-start.1) | collective-permute-done | bytes 27680 | tf_op jit(solution)/shard_map/ppermute | solution.py:283
  24.4 0.7 copy-done.6
  25.1 10.2 %attend.1 = (bf16[6,84,384]{2,1,0:T(8,128)(2,1)S(1)}, bf16[1280,128]{1,0:T(8,128)(2,1)}) custom-call(s32[8]{0:T(128)S(1)} %pad_add_fusion.meta_ref, bf16[6,84,192]{2,1,0:T(8,128)(2,1)S(1)} %copy-done.1, bf16[6,84,192]{2,1,0:T(8,128)(2,1)S(1)} %copy-done.2, bf16[3,84,384]{2,1,0:T(8,128)(2,1)S(1)} %collective-permute-done.up_ref, ...), custom_call_target="tpu_custom_call" | custom-call | flops 2000000000 | bytes 4000000 | tf_op jit(solution)/shard_map/attend/pallas_call | solution.py:215
  35.3 6.7 %all-to-all-start = ((bf16[32,40,128]{2,1,0:T(8,128)(2,1)}), bf16[32,40,128]{2,1,0:T(8,128)(2,1)S(1)}, u32[]{:S(2)}, u32[]{:S(2)}) async-start(bf16[32,40,128]{2,1,0:T(8,128)(2,1)} %bitcast.5), calls=%async_computation | async-start | bytes 655360 | tf_op jit(solution)/shard_map/all_to_all | solution.py:288
  42.0 3.5 %collective-permute-start.2 = (bf16[6,6,384]{2,1,0:T(8,128)(2,1)S(1)}, bf16[6,6,384]{2,1,0:T(8,128)(2,1)S(1)}, u32[]{:S(2)}, u32[]{:S(2)}) collective-permute-start(bf16[6,6,384]{2,1,0:T(8,128)(2,1)S(1)} %slice.38), channel_id=1, source_target_pairs={{0,1},{1,2},{2,3},{3,4},{4,5},{5,6},{6,7},{7,8},{8,9},{9,10},{10,1... | collective-permute-start | bytes 82952 | tf_op jit(solution)/shard_map/ppermute | solution.py:283
  45.6 5.3 %all-to-all-done = bf16[32,40,128]{2,1,0:T(8,128)(2,1)S(1)} async-done(((bf16[32,40,128]{2,1,0:T(8,128)(2,1)}), bf16[32,40,128]{2,1,0:T(8,128)(2,1)S(1)}, u32[]{:S(2)}, u32[]{:S(2)}) %all-to-all-start) | async-done | bytes 327712 | tf_op jit(solution)/shard_map/all_to_all | solution.py:288
  50.9 0.1 reduce_sum.24
  51.0 0.7 broadcast_in_dim.20
  51.7 11.2 %all-to-all-start.1 = ((bf16[16,40,128]{2,1,0:T(8,128)(2,1)}), bf16[16,40,128]{2,1,0:T(8,128)(2,1)S(1)}, u32[]{:S(2)}, u32[]{:S(2)}) async-start(bf16[16,40,128]{2,1,0:T(8,128)(2,1)} %broadcast_in_dim.20), calls=%async_computation.1 | async-start | bytes 327680 | tf_op jit(solution)/shard_map/all_to_all | solution.py:294
  62.9 0.1 pad_maximum_fusion
  63.0 2.3 %collective-permute-start.3 = (bf16[3,84,384]{2,1,0:T(8,128)(2,1)S(1)}, bf16[3,84,384]{2,1,0:T(8,128)(2,1)S(1)}, u32[]{:S(2)}, u32[]{:S(2)}) collective-permute-start(bf16[3,84,384]{2,1,0:T(8,128)(2,1)S(1)} %get-tuple-element.30), channel_id=1, source_target_pairs={{0,32},{32,64},{64,96},{96,128},{128,160},{160,192},{192,224},{224... | collective-permute-start | bytes 580616 | tf_op jit(solution)/shard_map/ppermute | solution.py:283
  65.3 9.5 %all-to-all-done.1 = bf16[16,40,128]{2,1,0:T(8,128)(2,1)S(1)} async-done(((bf16[16,40,128]{2,1,0:T(8,128)(2,1)}), bf16[16,40,128]{2,1,0:T(8,128)(2,1)S(1)}, u32[]{:S(2)}, u32[]{:S(2)}) %all-to-all-start.1) | async-done | bytes 163872 | tf_op jit(solution)/shard_map/all_to_all | solution.py:294
  74.9 0.4 collective-permute-done.3
  75.3 0.8 broadcast_in_dim.21
  76.1 6.0 %all-to-all-start.2 = ((bf16[32,40,128]{2,1,0:T(8,128)(2,1)}), bf16[32,40,128]{2,1,0:T(8,128)(2,1)S(1)}, u32[]{:S(2)}, u32[]{:S(2)}) async-start(bf16[32,40,128]{2,1,0:T(8,128)(2,1)} %broadcast_in_dim.21), calls=%async_computation.2 | async-start | bytes 655360 | tf_op jit(solution)/shard_map/all_to_all | solution.py:294
  82.0 0.1 maximum_convert_fusion
  82.1 1.1 %fusion = (bf16[6,84,192]{2,1,0:T(8,128)(2,1)}, bf16[6,84,192]{2,1,0:T(8,128)(2,1)}) fusion(f32[6,84,384]{2,1,0:T(8,128)S(1)} %maximum_convert_fusion, bf16[6,84,192]{2,1,0:T(8,128)(2,1)S(1)} %copy-done.2, bf16[6,84,192]{2,1,0:T(8,128)(2,1)S(1)} %copy-done.1), kind=kLoop, calls=%fused_computation.1 | loop fusion | flops 580608 | bytes 1548288 | tf_op jit(solution)/shard_map/convert_element_type | solution.py:330
  83.2 7.9 %all-to-all-done.2 = bf16[32,40,128]{2,1,0:T(8,128)(2,1)S(1)} async-done(((bf16[32,40,128]{2,1,0:T(8,128)(2,1)}), bf16[32,40,128]{2,1,0:T(8,128)(2,1)S(1)}, u32[]{:S(2)}, u32[]{:S(2)}) %all-to-all-start.2) | async-done | bytes 327712 | tf_op jit(solution)/shard_map/all_to_all | solution.py:294
  91.1 1.1 %finish.1 = (f32[192,576]{1,0:T(8,128)}, f32[192,192]{1,0:T(8,128)}, f32[48,253]{1,0:T(8,128)}, f32[1,192]{1,0:T(1,128)}) custom-call(bf16[1280,128]{1,0:T(8,128)(2,1)S(1)} %bitcast.13), custom_call_target="tpu_custom_call" | custom-call | flops 1000000 | bytes 1000000 | tf_op jit(solution)/shard_map/finish/pallas_call | solution.py:265
  (18 shorter events, 0.1 us)
Async XLA Ops:
  0.6 13.9 %copy-start = (s32[16,224]{1,0:T(8,128)S(1)}, s32[16,224]{1,0:T(8,128)}, u32[]{:S(2)}) copy-start(s32[16,224]{1,0:T(8,128)} %param.12) | copy-start | bytes 43012
  0.6 13.9 %copy-start.2 = (bf16[6,84,192]{2,1,0:T(8,128)(2,1)S(1)}, bf16[6,84,192]{2,1,0:T(8,128)(2,1)}, u32[]{:S(2)}) copy-start(bf16[6,84,192]{2,1,0:T(8,128)(2,1)} %g_ref.1) | copy-start | bytes 580612
  0.7 1.0 %slice-start = ((bf16[6,84,192]{2,1,0:T(8,128)(2,1)}), bf16[3,84,192]{2,1,0:T(8,128)(2,1)S(1)}, s32[]{:S(2)}) async-start(bf16[6,84,192]{2,1,0:T(8,128)(2,1)} %s_ref.1), calls=%async_computation.3 | async-start | bytes 270336 | tf_op jit(solution)/shard_map/slice | solution.py:311
  0.7 1.1 %slice-start.1 = ((bf16[6,84,192]{2,1,0:T(8,128)(2,1)}), bf16[3,84,192]{2,1,0:T(8,128)(2,1)S(1)}, s32[]{:S(2)}) async-start(bf16[6,84,192]{2,1,0:T(8,128)(2,1)} %g_ref.1), calls=%async_computation.4 | async-start | bytes 270336 | tf_op jit(solution)/shard_map/slice | solution.py:311
  1.7 12.8 %copy-start.1 = (bf16[6,84,192]{2,1,0:T(8,128)(2,1)S(1)}, bf16[6,84,192]{2,1,0:T(8,128)(2,1)}, u32[]{:S(2)}) copy-start(bf16[6,84,192]{2,1,0:T(8,128)(2,1)} %s_ref.1) | copy-start | bytes 580612
  1.7 22.7 %copy-start.3 = (bf16[192,576]{1,0:T(8,128)(2,1)S(1)}, bf16[192,576]{1,0:T(8,128)(2,1)}, u32[]{:S(2)}) copy-start(bf16[192,576]{1,0:T(8,128)(2,1)} %wqkv_ref.1) | copy-start | bytes 663556
  1.8 16.3 %collective-permute-start = (bf16[3,84,384]{2,1,0:T(8,128)(2,1)S(1)}, bf16[3,84,384]{2,1,0:T(8,128)(2,1)S(1)}, u32[]{:S(2)}, u32[]{:S(2)}) collective-permute-start(bf16[3,84,384]{2,1,0:T(8,128)(2,1)S(1)} %pad_maximum_fusion.1), channel_id=1, source_target_pairs={{0,480},{32,0},{64,32},{96,64},{128,96},{160,128},{192,160},{224,1... | collective-permute-start | bytes 580616 | tf_op jit(solution)/shard_map/ppermute | solution.py:283
  14.5 9.9 %copy-start.4 = (bf16[192,192]{1,0:T(8,128)(2,1)S(1)}, bf16[192,192]{1,0:T(8,128)(2,1)}, u32[]{:S(2)}) copy-start(bf16[192,192]{1,0:T(8,128)(2,1)} %wproj_ref.1) | copy-start | bytes 221188
  18.2 6.2 %copy-start.5 = (f32[8,6,253]{2,0,1:T(8,128)S(1)}, f32[8,6,253]{2,0,1:T(8,128)}, u32[]{:S(2)}) copy-start(f32[8,6,253]{2,0,1:T(8,128)} %param.11) | copy-start | bytes 145732
  18.3 6.2 %collective-permute-start.1 = (bf16[6,6,384]{2,1,0:T(8,128)(2,1)S(1)}, bf16[6,6,384]{2,1,0:T(8,128)(2,1)S(1)}, u32[]{:S(2)}, u32[]{:S(2)}) collective-permute-start(bf16[6,6,384]{2,1,0:T(8,128)(2,1)S(1)} %pad_maximum_fusion.2), channel_id=1, source_target_pairs={{0,31},{1,0},{2,1},{3,2},{4,3},{5,4},{6,5},{7,6},{8,7},{9,8},{10,9... | collective-permute-start | bytes 82952 | tf_op jit(solution)/shard_map/ppermute | solution.py:283
  24.4 0.7 copy-start.6
  35.3 15.7 %all-to-all-start = ((bf16[32,40,128]{2,1,0:T(8,128)(2,1)}), bf16[32,40,128]{2,1,0:T(8,128)(2,1)S(1)}, u32[]{:S(2)}, u32[]{:S(2)}) async-start(bf16[32,40,128]{2,1,0:T(8,128)(2,1)} %bitcast.5), calls=%async_computation | async-start | bytes 655360 | tf_op jit(solution)/shard_map/all_to_all | solution.py:288
  42.0 9.0 %collective-permute-start.2 = (bf16[6,6,384]{2,1,0:T(8,128)(2,1)S(1)}, bf16[6,6,384]{2,1,0:T(8,128)(2,1)S(1)}, u32[]{:S(2)}, u32[]{:S(2)}) collective-permute-start(bf16[6,6,384]{2,1,0:T(8,128)(2,1)S(1)} %slice.38), channel_id=1, source_target_pairs={{0,1},{1,2},{2,3},{3,4},{4,5},{5,6},{6,7},{7,8},{8,9},{9,10},{10,1... | collective-permute-start | bytes 82952 | tf_op jit(solution)/shard_map/ppermute | solution.py:283
  51.7 23.1 %all-to-all-start.1 = ((bf16[16,40,128]{2,1,0:T(8,128)(2,1)}), bf16[16,40,128]{2,1,0:T(8,128)(2,1)S(1)}, u32[]{:S(2)}, u32[]{:S(2)}) async-start(bf16[16,40,128]{2,1,0:T(8,128)(2,1)} %broadcast_in_dim.20), calls=%async_computation.1 | async-start | bytes 327680 | tf_op jit(solution)/shard_map/all_to_all | solution.py:294
  63.0 12.3 %collective-permute-start.3 = (bf16[3,84,384]{2,1,0:T(8,128)(2,1)S(1)}, bf16[3,84,384]{2,1,0:T(8,128)(2,1)S(1)}, u32[]{:S(2)}, u32[]{:S(2)}) collective-permute-start(bf16[3,84,384]{2,1,0:T(8,128)(2,1)S(1)} %get-tuple-element.30), channel_id=1, source_target_pairs={{0,32},{32,64},{64,96},{96,128},{128,160},{160,192},{192,224},{224... | collective-permute-start | bytes 580616 | tf_op jit(solution)/shard_map/ppermute | solution.py:283
  76.1 15.1 %all-to-all-start.2 = ((bf16[32,40,128]{2,1,0:T(8,128)(2,1)}), bf16[32,40,128]{2,1,0:T(8,128)(2,1)S(1)}, u32[]{:S(2)}, u32[]{:S(2)}) async-start(bf16[32,40,128]{2,1,0:T(8,128)(2,1)} %broadcast_in_dim.21), calls=%async_computation.2 | async-start | bytes 655360 | tf_op jit(solution)/shard_map/all_to_all | solution.py:294

commit v4 on v3

--- a/solution.py
+++ b/solution.py
@@ -23,11 +23,12 @@
 ROWS = 1280
 VM_ATTEND = 28
 VM_FINISH = 8
+VM_BIAS = 10
 LAT = ("y_lo", "z_hi", "z_lo")
 LON = ("y_hi", "x", "core")
 PARTS = (2, 4, 2, 4, 4, 2)
 SLICED = ("y_lo", "z_lo", "x", "core")
-WHOLE = (("z_hi", "y_hi"),)
+WHOLE = ("z_hi", "y_hi")
 highest = lax.Precision.HIGHEST
 f32 = jnp.float32
 bf16 = jnp.bfloat16
@@ -61,13 +62,9 @@
     return hit.astype(f32)
 
 
-def kernel(windows, meta_ref, s_ref, g_ref, up_ref, side_ref, gain_ref, wqkv_ref, wproj_ref, table_ref,
-           both_ref, grads_ref,
-           xs, gs, tab, tilt, span, bias, un, nm, inv, q_s, k_s, v_s, dm_s, mix, dq_s, dk_s, dv_s, fold):
+def bias_kernel(table_ref, last_ref, bias, tab, tilt, span):
     half_lat = WIN_LAT // 2
-    half_lon = WIN_LON // 2
     kinds = table_ref.shape[0] // HEADS
-
     tab[...] = jnp.zeros_like(tab)
     tab[:, :table_ref.shape[1]] = table_ref[...]
     for c in range(PITCH):
@@ -78,7 +75,7 @@
     span[...] = nn(jnp.concatenate([tilt[0], tilt[1]], axis=1), pattern, precision=highest)
     slot = iota((PITCH, LANES), 1)
     open_slot = (slot % PITCH < WIN_LON) & (slot < TOK)
-    split = meta_ref[windows] > 0
+    split = last_ref[0] > 0
 
     def spread(n, carry):
         wide = span[pl.ds(pl.multiple_of(n * PITCH, PITCH), PITCH), :]
@@ -91,6 +88,32 @@
         return carry
 
     lax.fori_loop(0, kinds * HEADS, spread, 0, unroll=True)
+
+
+def bias_of(table, last):
+    vm = pl.BlockSpec(memory_space=pltpu.VMEM)
+    kh = table.shape[0]
+    return pl.pallas_call(
+        bias_kernel,
+        out_shape=jax.ShapeDtypeStruct((kh // HEADS, HEADS * TOK, LANES), f32),
+        in_specs=[vm, pl.BlockSpec(memory_space=pltpu.SMEM)],
+        out_specs=vm,
+        scratch_shapes=[
+            pltpu.VMEM((kh, SPAN), f32), pltpu.VMEM((2, kh * PITCH, LANES), f32), pltpu.VMEM((kh * PITCH, SPAN), f32),
+        ],
+        cost_estimate=pl.CostEstimate(flops=600_000_000, bytes_accessed=2_500_000, transcendentals=0),
+        compiler_params=pltpu.CompilerParams(vmem_limit_bytes=VM_BIAS << 20),
+        name="bias",
+    )(table, last)
+
+
+def kernel(windows, kinds, meta_ref, s_ref, g_ref, up_ref, side_ref, corner_ref, gain_ref, wqkv_ref, wproj_ref, bias,
+           both_ref, grads_ref,
+           xs, gs, tilt, un, nm, inv, q_s, k_s, v_s, dm_s, mix, dq_s, dk_s, dv_s, fold):
+    half_lat = WIN_LAT // 2
+    half_lon = WIN_LON // 2
+
+    pattern = base_pattern()
     fold[...] = jnp.zeros_like(fold)
 
     xs[...] = jnp.zeros_like(xs)
@@ -108,7 +131,7 @@
                 else:
                     dst[at:at + inside, :] = up_ref[r - half_lat, start:start + inside, lo:lo + D]
                     if inside < WIN_LON:
-                        dst[at + inside:at + WIN_LON, :] = side_ref[r, :, lo:lo + D]
+                        dst[at + inside:at + WIN_LON, :] = corner_ref[r - half_lat, :, lo:lo + D]
 
     gain = gain_ref[...]
     x = xs[...].astype(f32)
@@ -173,7 +196,7 @@
     gp = tn(mix[...], gs[...]).astype(bf16)
     d_normed = nt(dq_s[...], wq) + nt(dk_s[...], wk) + nt(dv_s[...], wv)
     gq = []
-    for i, d in enumerate((dq_s, dk_s, dv_s)):
+    for d in (dq_s, dk_s, dv_s):
         gq.append(tn(nm[...], d[...]).astype(bf16))
     gq = jnp.concatenate(gq, axis=1)
     for b in range(4):
@@ -207,29 +230,27 @@
         grads_ref[at:at + kinds * HEADS, :] = total[:, half * LANES:(half + 1) * LANES].astype(bf16)
 
 
-def attend(meta, s, g, up, side, gain, w_qkv, w_proj, table):
+def attend(kinds, s, g, up, side, corner, gain, w_qkv, w_proj, bias):
     windows = s.shape[1] // WIN_LON
     n = windows * TOK
     vm = pl.BlockSpec(memory_space=pltpu.VMEM)
-    kh = table.shape[0]
+    kh = bias.shape[0] * HEADS
     return pl.pallas_call(
-        functools.partial(kernel, windows),
+        functools.partial(kernel, windows, bias.shape[0]),
         out_shape=(
             jax.ShapeDtypeStruct(s.shape[:2] + (2 * D,), bf16),
             jax.ShapeDtypeStruct((ROWS, LANES), bf16),
         ),
-        in_specs=[pl.BlockSpec(memory_space=pltpu.SMEM)] + [vm] * 8,
+        in_specs=[pl.BlockSpec(memory_space=pltpu.SMEM)] + [vm] * 9,
         out_specs=(vm,) * 2,
         scratch_shapes=[
-            pltpu.VMEM((n, D), bf16), pltpu.VMEM((n, D), bf16), pltpu.VMEM((kh, SPAN), f32),
-            pltpu.VMEM((2, kh * PITCH, LANES), f32), pltpu.VMEM((kh * PITCH, SPAN), f32),
-            pltpu.VMEM((kh // HEADS, HEADS * TOK, LANES), f32),
+            pltpu.VMEM((n, D), bf16), pltpu.VMEM((n, D), bf16), pltpu.VMEM((2, kh * PITCH, LANES), f32),
             pltpu.VMEM((n, D), f32), pltpu.VMEM((n, D), bf16), pltpu.VMEM((n, 1), f32),
         ] + [pltpu.VMEM((n, D), bf16)] * 8 + [pltpu.VMEM((kh * PITCH, SPAN), f32)],
         cost_estimate=pl.CostEstimate(flops=2_000_000_000, bytes_accessed=4_000_000, transcendentals=500_000),
         compiler_params=pltpu.CompilerParams(vmem_limit_bytes=VM_ATTEND << 20),
         name="attend",
-    )(meta, s, g, up, side, gain, w_qkv, w_proj, table)
+    )(kinds, s, g, up, side, corner, gain, w_qkv, w_proj, bias)
 
 
 def finish_kernel(grads_ref, gq_ref, gp_ref, gt_ref, gg_ref):
@@ -283,49 +304,51 @@
     return lax.ppermute(value, axis, [(i, (i + steps) % count) for i in range(count)])
 
 
-def spread_sum(part, axes):
-    n = lax.axis_size(axes)
-    got = lax.all_to_all(part.reshape(n, -1, LANES), axes, 0, 0, tiled=True)
+def exchange(part, axes):
+    return lax.all_to_all(part, axes, 0, 0, tiled=True)
+
+
+def whole_sum(got):
     return jnp.sum(got.astype(f32), axis=0).astype(bf16)
 
 
-def collect(part, axes):
-    n = lax.axis_size(axes)
-    return lax.all_to_all(jnp.broadcast_to(part[None], (n,) + part.shape), axes, 0, 0, tiled=True)
-
-
-def total_of(packed, ahead, further):
-    part = spread_sum(packed, SLICED)
-    part, ahead = lax.optimization_barrier((part, ahead))
-    for axes in WHOLE:
-        part = jnp.sum(collect(part, axes).astype(f32), axis=0).astype(bf16)
-    part, ahead = lax.optimization_barrier((part, further(ahead)))
-    return collect(part, SLICED).reshape(-1, LANES), ahead
+def copies(part, axes):
+    return jnp.broadcast_to(part[None], (lax.axis_size(axes),) + part.shape)
+
+
+def total_of(packed):
+    part = exchange(packed.reshape(lax.axis_size(SLICED), -1, LANES), SLICED)
+    part = whole_sum(part)
+    part = exchange(copies(part, WHOLE), WHOLE)
+    part = whole_sum(part)
+    part = exchange(copies(part, SLICED), SLICED)
+    return part.reshape(-1, LANES)
 
 
 def on_device(state_grid, norm_gain, w_qkv, w_proj, bias_table, window_kind, cotangent):
-    rows_dev, cols_dev, channels = state_grid.shape
+    _, cols_dev, channels = state_grid.shape
     half_lat, half_lon = WIN_LAT // 2, WIN_LON // 2
     lat, lon = lax.axis_index(LAT), lax.axis_index(LON)
     windows = cols_dev // WIN_LON
     joint = jnp.concatenate([state_grid[:half_lat], cotangent[:half_lat]], axis=2)
+    side = jnp.concatenate([state_grid[half_lat:, :half_lon], cotangent[half_lat:, :half_lon]], axis=2)
     up = shifted(joint, LAT, -1)
-    side = jnp.concatenate([state_grid[half_lat:, :half_lon], cotangent[half_lat:, :half_lon]], axis=2)
-    side = shifted(jnp.concatenate([side, up[:, :half_lon]], axis=0), LON, -1)
+    lats, lons = lax.axis_size(LAT), lax.axis_size(LON)
+    before = [(i * lons + j, (i - 1) % lats * lons + (j - 1) % lons) for i in range(lats) for j in range(lons)]
+    corner = lax.ppermute(joint[:, :half_lon], LAT + LON, before)
+    side = shifted(side, LON, -1)
     kinds = lax.dynamic_slice(window_kind, (lat, lon * windows), (1, windows))[0]
     last = (lat == lax.axis_size(LAT) - 1).astype(jnp.int32)
-    meta = jnp.concatenate([kinds, last[None]])
     kind_count, heads, extent = bias_table.shape
     table = bias_table.transpose(1, 0, 2).reshape(heads * kind_count, extent)
-    both, packed = attend(meta, state_grid, cotangent, up, side, norm_gain.reshape(1, -1), w_qkv, w_proj, table)
+    both, packed = attend(
+        kinds, state_grid, cotangent, up, side, corner, norm_gain.reshape(1, -1), w_qkv, w_proj, bias_of(table, last[None])
+    )
     moved = shifted(both[:, -half_lon:], LON, 1)
-
-    def up_to_rows(moved):
-        placed = jnp.concatenate([moved, both[:, :-half_lon]], axis=1)
-        return placed[:half_lat], shifted(placed[half_lat:], LAT, 1)
-
-    summed, (stay, lower) = total_of(packed, moved, up_to_rows)
-    own = jnp.concatenate([lower, stay], axis=0).astype(f32)
+    placed = jnp.concatenate([moved, both[:, :-half_lon]], axis=1)
+    lower = shifted(placed[half_lat:], LAT, 1)
+    summed = total_of(packed)
+    own = jnp.concatenate([lower, placed[:half_lat]], axis=0).astype(f32)
     out_field = (state_grid.astype(f32) + own[:, :, :channels]).astype(bf16)
     d_field = (cotangent.astype(f32) + own[:, :, channels:]).astype(bf16)
     gq, gp, gt, gg = finish(summed, heads * kind_count, extent)

time: 92.7 us -> 91.2 us (0.984)
  blocking collectives: 0 us -> 12.7 us
  waiting for transfers between devices: 29.4 us -> 17.2 us
  starting transfers between devices: 45.8 us -> 41.4 us
  local copies, waits for them, and re-layouts: 3.36 us -> 5.75 us
    all_to_all x3 -> x2, waiting for transfers between devices: 22.8 us -> 8.75 us  [exchange(): return lax.all_to_all(part, axes, 0, 0, tiled=True)]
    all_to_all x0 -> x1, blocking collectives: none -> 12.7 us  [exchange(): return lax.all_to_all(part, axes, 0, 0, tiled=True)]
    all_to_all x3 -> x2, starting transfers between devices: 23.9 us -> 13.1 us  [exchange(): return lax.all_to_all(part, axes, 0, 0, tiled=True)]
    ppermute x0 -> x1, starting transfers between devices: none -> 7.32 us  [on_device(): corner = lax.ppermute(joint[:, :half_lon], LAT + LON, before)]
    ppermute x4, waiting for transfers between devices: 6.58 us -> 8.47 us  [shifted(): lax.ppermute(value, axis, [(i, (i + steps) % count) for i in range(count)])]
    pallas_call x1 -> x2, Pallas kernels: 10.2 us -> 10.1 us  [the longest x1 7.94 us: attend(): pl.pallas_call(functools.partial(kernel, windows, bias.shape[0]), out_sha...]
  transfers between devices with their start and end apart: 7 -> 7, of which waited for: 6 -> 2; matrix products, arithmetic and copies ran while one was open for 2% -> 5% of each run, Pallas kernels for 0% -> 2%
where the time goes in v4:
time: 91.2 us; the launch traced here: 90.7 us
  starting transfers between devices  41.4 us (45%)
  waiting for transfers between devices  17.2 us (19%)
  blocking collectives  12.7 us (14%)
  Pallas kernels  11.2 us (12%)
  local copies, waits for them, and re-layouts  5.75 us (6%)
  other arithmetic  1.53 us (2%)
    ppermute x4, starting transfers between devices, shifted(): lax.ppermute(value, axis, [(i, (i + steps) % count) for i in range(count)])  21 us
    all_to_all x2, starting transfers between devices, exchange(): return lax.all_to_all(part, axes, 0, 0, tiled=True)  13.1 us
    all_to_all x1, blocking collectives, exchange(): return lax.all_to_all(part, axes, 0, 0, tiled=True)  12.7 us
    all_to_all x2, waiting for transfers between devices, exchange(): return lax.all_to_all(part, axes, 0, 0, tiled=True)  8.75 us
    ppermute x4, waiting for transfers between devices, shifted(): lax.ppermute(value, axis, [(i, (i + steps) % count) for i in range(count)])  8.47 us
    pallas_call x1, Pallas kernels, attend(): pl.pallas_call(functools.partial(kernel, windows, bias.shape[0]), out_sha...  7.94 us
    ppermute x1, starting transfers between devices, on_device(): corner = lax.ppermute(joint[:, :half_lon], LAT + LON, before)  7.32 us
    pallas_call x1, Pallas kernels, bias_of(): pl.pallas_call(bias_kernel, out_shape=jax.ShapeDtypeStruct((kh // HEADS,...  2.14 us
  transfers between devices with their start and end apart: 7, of which 2 were waited for; matrix products, arithmetic and copies ran while one was open for 5% of the time, Pallas kernels for 2%

profile of v4, /device:TPU:1, one launch (start us, length us, event | category | flops | bytes accessed | tf_op | source)
XLA Modules:
  0.0 90.7 jit_solution(2919704946120384076)
XLA Ops:
  0.6 0.0 copy-start
  0.6 0.0 copy-start.1
  0.7 0.0 copy-start.2
  0.7 0.8 slice.35
  1.5 0.7 slice.36
  2.2 0.1 pad_maximum_fusion.2
  2.3 8.7 %collective-permute-start.1 = (bf16[3,6,384]{2,1,0:T(8,128)(2,1)S(1)}, bf16[3,6,384]{2,1,0:T(8,128)(2,1)S(1)}, u32[]{:S(2)}, u32[]{:S(2)}) collective-permute-start(bf16[3,6,384]{2,1,0:T(8,128)(2,1)S(1)} %pad_maximum_fusion.2), channel_id=1, source_target_pairs={{0,31},{1,0},{2,1},{3,2},{4,3},{5,4},{6,5},{7,6},{8,7},{9,8},{10,9... | collective-permute-start | bytes 41480 | tf_op jit(solution)/shard_map/ppermute | solution.py:304
  11.0 0.9 %slice.33 = bf16[3,84,192]{2,1,0:T(8,128)(2,1)S(1)} slice(bf16[6,84,192]{2,1,0:T(8,128)(2,1)} %s_ref.1), slice={[0:3], [0:84], [0:192]} | slice | bytes 193536 | tf_op jit(solution)/shard_map/slice | solution.py:333
  11.9 0.9 %slice.34 = bf16[3,84,192]{2,1,0:T(8,128)(2,1)S(1)} slice(bf16[6,84,192]{2,1,0:T(8,128)(2,1)} %g_ref.1), slice={[0:3], [0:84], [0:192]} | slice | bytes 193536 | tf_op jit(solution)/shard_map/slice | solution.py:333
  12.9 0.1 pad_maximum_fusion.1
  13.0 6.3 %collective-permute-start = (bf16[3,84,384]{2,1,0:T(8,128)(2,1)S(1)}, bf16[3,84,384]{2,1,0:T(8,128)(2,1)S(1)}, u32[]{:S(2)}, u32[]{:S(2)}) collective-permute-start(bf16[3,84,384]{2,1,0:T(8,128)(2,1)S(1)} %pad_maximum_fusion.1), channel_id=1, source_target_pairs={{0,480},{32,0},{64,32},{96,64},{128,96},{160,128},{192,160},{224,1... | collective-permute-start | bytes 580616 | tf_op jit(solution)/shard_map/ppermute | solution.py:304
  19.3 0.1 fusion.5
  19.4 7.3 %collective-permute-start.2 = (bf16[3,6,384]{2,1,0:T(8,128)(2,1)S(1)}, bf16[3,6,384]{2,1,0:T(8,128)(2,1)S(1)}, u32[]{:S(2)}, u32[]{:S(2)}) collective-permute-start(bf16[3,6,384]{2,1,0:T(8,128)(2,1)S(1)} %fusion.5), channel_id=1, source_target_pairs={{0,511},{1,480},{2,481},{3,482},{4,483},{5,484},{6,485},{7,486},{8... | collective-permute-start | bytes 41480 | tf_op jit(solution)/shard_map/ppermute | solution.py:338
  26.7 0.1 dynamic-slice_bitcast_fusion.meta_ref
  26.8 0.8 copy-done.3
  27.6 2.1 %bias.1 = f32[8,576,128]{2,1,0:T(8,128)S(1)} custom-call(f32[48,253]{1,0:T(8,128)S(1)} %bitcast.15, s32[1]{0:T(128)} %bitcast.4.last_ref), custom_call_target="tpu_custom_call" | custom-call | flops 600000000 | bytes 2500000 | tf_op jit(solution)/shard_map/bias/pallas_call | solution.py:96
  29.8 0.0 collective-permute-done.1.side_ref
  29.9 7.9 %attend.1 = (bf16[6,84,384]{2,1,0:T(8,128)(2,1)S(1)}, bf16[1280,128]{1,0:T(8,128)(2,1)S(1)}) custom-call(s32[7]{0:T(128)S(1)} %dynamic-slice_bitcast_fusion.meta_ref, bf16[6,84,192]{2,1,0:T(8,128)(2,1)S(1)} %copy-done.1, bf16[6,84,192]{2,1,0:T(8,128)(2,1)S(1)} %copy-done.2, bf16[3,84,384]{2,1,0:T(8,128)(2,1)S(1)} %collective-permute-done.up_ref, ...), custom_call_target="tpu_custom_call" | custom-call | flops 2000000000 | bytes 4000000 | tf_op jit(solution)/shard_map/attend/pallas_call | solution.py:238
  37.8 12.7 %all_to_all.15 = bf16[32,40,128]{2,1,0:T(8,128)(2,1)S(1)} all-to-all(bf16[32,40,128]{2,1,0:T(8,128)(2,1)S(1)} %bitcast.14), channel_id=1, replica_groups=mesh['y_lo'=2,'z_hi'=4,'z_lo'=2,'y_hi'=4,'x'=4,'core'=2] {'y_lo','z_lo',..., dimensions={0} | all-to-all | bytes 655360 | tf_op jit(solution)/shard_map/all_to_all | solution.py:308
  50.5 0.1 reduce_sum.24
  50.5 0.7 broadcast_in_dim.19
  51.2 7.9 %all-to-all-start.1 = ((bf16[16,40,128]{2,1,0:T(8,128)(2,1)}), bf16[16,40,128]{2,1,0:T(8,128)(2,1)S(1)}, u32[]{:S(2)}, u32[]{:S(2)}) async-start(bf16[16,40,128]{2,1,0:T(8,128)(2,1)} %broadcast_in_dim.19), calls=%async_computation.1 | async-start | bytes 327680 | tf_op jit(solution)/shard_map/all_to_all | solution.py:308
  59.1 2.6 %collective-permute-start.3 = (bf16[6,6,384]{2,1,0:T(8,128)(2,1)S(1)}, bf16[6,6,384]{2,1,0:T(8,128)(2,1)S(1)}, u32[]{:S(2)}, u32[]{:S(2)}) collective-permute-start(bf16[6,6,384]{2,1,0:T(8,128)(2,1)S(1)} %slice.38), channel_id=1, source_target_pairs={{0,1},{1,2},{2,3},{3,4},{4,5},{5,6},{6,7},{7,8},{8,9},{9,10},{10,1... | collective-permute-start | bytes 82952 | tf_op jit(solution)/shard_map/ppermute | solution.py:304
  61.8 8.7 %all-to-all-done.1 = bf16[16,40,128]{2,1,0:T(8,128)(2,1)S(1)} async-done(((bf16[16,40,128]{2,1,0:T(8,128)(2,1)}), bf16[16,40,128]{2,1,0:T(8,128)(2,1)S(1)}, u32[]{:S(2)}, u32[]{:S(2)}) %all-to-all-start.1) | async-done | bytes 163872 | tf_op jit(solution)/shard_map/all_to_all | solution.py:308
  70.6 0.8 broadcast_in_dim.20
  71.3 5.3 %all-to-all-start.2 = ((bf16[32,40,128]{2,1,0:T(8,128)(2,1)}), bf16[32,40,128]{2,1,0:T(8,128)(2,1)S(1)}, u32[]{:S(2)}, u32[]{:S(2)}) async-start(bf16[32,40,128]{2,1,0:T(8,128)(2,1)} %broadcast_in_dim.20), calls=%async_computation.2 | async-start | bytes 655360 | tf_op jit(solution)/shard_map/all_to_all | solution.py:308
  76.6 0.1 fusion.4
  76.7 3.3 %collective-permute-start.4 = (bf16[3,84,384]{2,1,0:T(8,128)(2,1)S(1)}, bf16[3,84,384]{2,1,0:T(8,128)(2,1)S(1)}, u32[]{:S(2)}, u32[]{:S(2)}) collective-permute-start(bf16[3,84,384]{2,1,0:T(8,128)(2,1)S(1)} %fusion.4), channel_id=1, source_target_pairs={{0,32},{32,64},{64,96},{96,128},{128,160},{160,192},{192,224},{224... | collective-permute-start | bytes 580616 | tf_op jit(solution)/shard_map/ppermute | solution.py:304
  80.0 8.5 %collective-permute-done.4 = bf16[3,84,384]{2,1,0:T(8,128)(2,1)S(1)} collective-permute-done((bf16[3,84,384]{2,1,0:T(8,128)(2,1)S(1)}, bf16[3,84,384]{2,1,0:T(8,128)(2,1)S(1)}, u32[]{:S(2)}, u32[]{:S(2)}) %collective-permute-start.4) | collective-permute-done | bytes 193568 | tf_op jit(solution)/shard_map/ppermute | solution.py:304
  88.5 0.1 fusion.3
  88.5 1.0 %fusion = (bf16[6,84,192]{2,1,0:T(8,128)(2,1)}, bf16[6,84,192]{2,1,0:T(8,128)(2,1)}) fusion(f32[6,84,384]{2,1,0:T(8,128)S(1)} %fusion.3, bf16[6,84,192]{2,1,0:T(8,128)(2,1)S(1)} %copy-done.2, bf16[6,84,192]{2,1,0:T(8,128)(2,1)S(1)} %copy-done.1), kind=kLoop, calls=%fused_computation.1 | loop fusion | flops 580608 | bytes 1548288 | tf_op jit(solution)/shard_map/convert_element_type | solution.py:353
  89.6 1.1 %finish.1 = (f32[192,576]{1,0:T(8,128)}, f32[192,192]{1,0:T(8,128)}, f32[48,253]{1,0:T(8,128)}, f32[1,192]{1,0:T(1,128)}) custom-call(bf16[1280,128]{1,0:T(8,128)(2,1)S(1)} %bitcast.13), custom_call_target="tpu_custom_call" | custom-call | flops 1000000 | bytes 1000000 | tf_op jit(solution)/shard_map/finish/pallas_call | solution.py:286
  (17 shorter events, 0.1 us)
Async XLA Ops:
  0.6 26.1 %copy-start = (s32[16,224]{1,0:T(8,128)S(1)}, s32[16,224]{1,0:T(8,128)}, u32[]{:S(2)}) copy-start(s32[16,224]{1,0:T(8,128)} %param.12) | copy-start | bytes 43012
  0.6 29.2 %copy-start.1 = (bf16[6,84,192]{2,1,0:T(8,128)(2,1)S(1)}, bf16[6,84,192]{2,1,0:T(8,128)(2,1)}, u32[]{:S(2)}) copy-start(bf16[6,84,192]{2,1,0:T(8,128)(2,1)} %s_ref.1) | copy-start | bytes 580612
  0.7 29.2 %copy-start.2 = (bf16[6,84,192]{2,1,0:T(8,128)(2,1)S(1)}, bf16[6,84,192]{2,1,0:T(8,128)(2,1)}, u32[]{:S(2)}) copy-start(bf16[6,84,192]{2,1,0:T(8,128)(2,1)} %g_ref.1) | copy-start | bytes 580612
  0.7 29.2 %copy-start.5 = (bf16[192,192]{1,0:T(8,128)(2,1)S(1)}, bf16[192,192]{1,0:T(8,128)(2,1)}, u32[]{:S(2)}) copy-start(bf16[192,192]{1,0:T(8,128)(2,1)} %wproj_ref.1) | copy-start | bytes 221188
  0.7 29.2 %copy-start.4 = (bf16[192,576]{1,0:T(8,128)(2,1)S(1)}, bf16[192,576]{1,0:T(8,128)(2,1)}, u32[]{:S(2)}) copy-start(bf16[192,576]{1,0:T(8,128)(2,1)} %wqkv_ref.1) | copy-start | bytes 663556
  0.7 29.2 %copy-start.6 = (f32[192]{0:T(256)S(1)}, f32[192]{0:T(256)}, u32[]{:S(2)}) copy-start(f32[192]{0:T(256)} %param.8) | copy-start | bytes 2308
  2.3 27.5 %collective-permute-start.1 = (bf16[3,6,384]{2,1,0:T(8,128)(2,1)S(1)}, bf16[3,6,384]{2,1,0:T(8,128)(2,1)S(1)}, u32[]{:S(2)}, u32[]{:S(2)}) collective-permute-start(bf16[3,6,384]{2,1,0:T(8,128)(2,1)S(1)} %pad_maximum_fusion.2), channel_id=1, source_target_pairs={{0,31},{1,0},{2,1},{3,2},{4,3},{5,4},{6,5},{7,6},{8,7},{9,8},{10,9... | collective-permute-start | bytes 41480 | tf_op jit(solution)/shard_map/ppermute | solution.py:304
  13.0 16.8 %collective-permute-start = (bf16[3,84,384]{2,1,0:T(8,128)(2,1)S(1)}, bf16[3,84,384]{2,1,0:T(8,128)(2,1)S(1)}, u32[]{:S(2)}, u32[]{:S(2)}) collective-permute-start(bf16[3,84,384]{2,1,0:T(8,128)(2,1)S(1)} %pad_maximum_fusion.1), channel_id=1, source_target_pairs={{0,480},{32,0},{64,32},{96,64},{128,96},{160,128},{192,160},{224,1... | collective-permute-start | bytes 580616 | tf_op jit(solution)/shard_map/ppermute | solution.py:304
  19.4 10.4 %collective-permute-start.2 = (bf16[3,6,384]{2,1,0:T(8,128)(2,1)S(1)}, bf16[3,6,384]{2,1,0:T(8,128)(2,1)S(1)}, u32[]{:S(2)}, u32[]{:S(2)}) collective-permute-start(bf16[3,6,384]{2,1,0:T(8,128)(2,1)S(1)} %fusion.5), channel_id=1, source_target_pairs={{0,511},{1,480},{2,481},{3,482},{4,483},{5,484},{6,485},{7,486},{8... | collective-permute-start | bytes 41480 | tf_op jit(solution)/shard_map/ppermute | solution.py:338
  26.8 0.8 copy-start.3
  51.2 19.3 %all-to-all-start.1 = ((bf16[16,40,128]{2,1,0:T(8,128)(2,1)}), bf16[16,40,128]{2,1,0:T(8,128)(2,1)S(1)}, u32[]{:S(2)}, u32[]{:S(2)}) async-start(bf16[16,40,128]{2,1,0:T(8,128)(2,1)} %broadcast_in_dim.19), calls=%async_computation.1 | async-start | bytes 327680 | tf_op jit(solution)/shard_map/all_to_all | solution.py:308
  59.1 17.5 %collective-permute-start.3 = (bf16[6,6,384]{2,1,0:T(8,128)(2,1)S(1)}, bf16[6,6,384]{2,1,0:T(8,128)(2,1)S(1)}, u32[]{:S(2)}, u32[]{:S(2)}) collective-permute-start(bf16[6,6,384]{2,1,0:T(8,128)(2,1)S(1)} %slice.38), channel_id=1, source_target_pairs={{0,1},{1,2},{2,3},{3,4},{4,5},{5,6},{6,7},{7,8},{8,9},{9,10},{10,1... | collective-permute-start | bytes 82952 | tf_op jit(solution)/shard_map/ppermute | solution.py:304
  71.3 18.3 %all-to-all-start.2 = ((bf16[32,40,128]{2,1,0:T(8,128)(2,1)}), bf16[32,40,128]{2,1,0:T(8,128)(2,1)S(1)}, u32[]{:S(2)}, u32[]{:S(2)}) async-start(bf16[32,40,128]{2,1,0:T(8,128)(2,1)} %broadcast_in_dim.20), calls=%async_computation.2 | async-start | bytes 655360 | tf_op jit(solution)/shard_map/all_to_all | solution.py:308
  76.7 11.8 %collective-permute-start.4 = (bf16[3,84,384]{2,1,0:T(8,128)(2,1)S(1)}, bf16[3,84,384]{2,1,0:T(8,128)(2,1)S(1)}, u32[]{:S(2)}, u32[]{:S(2)}) collective-permute-start(bf16[3,84,384]{2,1,0:T(8,128)(2,1)S(1)} %fusion.4), channel_id=1, source_target_pairs={{0,32},{32,64},{64,96},{96,128},{128,160},{160,192},{192,224},{224... | collective-permute-start | bytes 580616 | tf_op jit(solution)/shard_map/ppermute | solution.py:304
